TPU v7x, 512 devices: a whole 4x4x16 slice. The times are simulated.
512 devices in a mesh: cuts: 32 (over z, core), row: 16 (over y, x).
Axes of the slice: x: 4, y: 4, z: 16, core: 2. Of those that a mesh axis runs over, the one named last changes fastest.
Arguments:
- field: float32 [2, 256, 256, 256], P(None, 'cuts', 'row'), may hold values from -6 to 6
- row_prop: float32 [2, 256, 256], replicated, may hold values from -0.25 to 0.25
- col_prop: float32 [2, 256, 256], replicated, may hold values from -0.25 to 0.25
- phase: float32 [256, 8192], P('cuts', 'row'), may hold values from -3.140625 to 3.140625
- energy: float32 [256, 8192], P('cuts', 'row'), may hold values from -6 to 6
- cells: int32 [256, 8192], P('cuts', 'row'), may hold values from 0 to 65535, as said below
- shifts: int32 [4], replicated, may hold values from 1 to 2, as said below
Outputs:
- field_out: float32 [2, 256, 256, 256], P(None, 'cuts', 'row')
- phase_out: float32 [256, 8192], P('cuts', 'row')
- energy_out: float32 [256, 8192], P('cuts', 'row')
- bunching: float32 [4, 2, 256], P(None, None, 'cuts')
Inputs may be any that keep to these rules, and one draw needn't show every extreme that they name: `cells`: electron j of a slice sits in a grid row from b * 16 to (b + 1) * 16 - 1, where b = j // 512. `shifts`: 2 slices slip in at least one period.
All inputs are finite; a program needn't handle non-finite values.
Results may differ from a plain program's by a relative error of at most 0.00021.
Values sent between devices are 32-bit elements; how exact they have to be, the bound alone decides.
A program may use at most 64 MiB of HBM per device.

v0:
```python
import jax
import jax.numpy as jnp
from jax import lax
from jax.experimental import pallas as pl
from jax.experimental.pallas import tpu as pltpu
from jax.sharding import PartitionSpec as P

F32 = jnp.float32
BF16 = jnp.bfloat16
MESH = pl.DeviceIdType.MESH
ELEC = 8192
PLANES = 16
CUTS = 32
SLOTS = 256
kick_rate = 0.5
source_gain = 0.5


def split(x):
    high = x.astype(BF16)
    return high, (x - high.astype(F32)).astype(BF16)


def kernel(shifts, field_in, row_in, col_in, phase_in, energy_in, cells_in,
           field_out, phase_out, energy_out, sums_out,
           own, halo, rowp, colp, ph_in, en_in, ce_in,
           mh, ml, ah, al,
           cell_f, row_i, col_i, onehot, fld, gx, gown, goth,
           samp, emit, state, xst, xce, rxst, rxce, rst, rce, efin, fin, rfld, rel, rsum,
           lsem, s_halo, r_halo, s_a2a, r_a2a, s_fwd, r_fwd, s_ex, r_ex,
           s_xst, r_xst, s_xce, r_xce, s_st, r_st, s_ce, r_ce,
           s_fld, r_fld, s_el, r_el, s_sum, r_sum):
    c = lax.axis_index("cuts")
    b = lax.axis_index("row")
    z = c // 2
    h = c % 2
    slot = z * 16 + b
    half = b // 8
    place = b % 8
    sends = []

    def coords(j, core):
        return (j // 16) * 2 + core, j % 16

    def remote(src, dst, ss, rs, dc, db):
        return pltpu.make_async_remote_copy(
            src_ref=src, dst_ref=dst, send_sem=ss, recv_sem=rs,
            device_id=(dc, db), device_id_type=MESH)

    def send(src, dst, ss, rs, dc, db, extra=None):
        here = (dc == c) & (db == b)
        there = jnp.logical_not(here)
        if extra is not None:
            here = here & extra
            there = there & extra

        @pl.when(there)
        def _():
            remote(src, dst, ss, rs, dc, db).start()

        @pl.when(here)
        def _():
            dst[...] = src[...]

        sends.append((there, src, dst, ss, rs))

    def sure_send(src, dst, ss, rs, dc, db):
        remote(src, dst, ss, rs, dc, db).start()
        sends.append((None, src, dst, ss, rs))

    def await_from(dst, ss, rs, dc, db):
        @pl.when(jnp.logical_not((dc == c) & (db == b)))
        def _():
            remote(dst, dst, ss, rs, dc, db).wait_recv()

    def sure_await(dst, ss, rs):
        remote(dst, dst, ss, rs, c, b).wait_recv()

    loads = [(field_in, own), (phase_in, ph_in), (energy_in, en_in), (cells_in, ce_in),
             (col_in, colp), (row_in, rowp)]
    loads = [pltpu.make_async_copy(src, dst, lsem.at[n]) for n, (src, dst) in enumerate(loads)]
    for copy in loads:
        copy.start()

    barrier = pltpu.get_barrier_semaphore()
    mine = 32 + h * 16 + b

    def greet(off, carry):
        peer = (mine + off) % 96
        dc = (z * 2 - 2 + peer // 16 + CUTS) % CUTS
        pl.semaphore_signal(barrier, inc=1, device_id=(dc, peer % 16), device_id_type=MESH)
        return carry

    lax.fori_loop(1, 96, greet, 0)

    for n in (1, 2, 3):
        loads[n].wait()
    for u in range(8):
        for i in range(4):
            lanes = slice(128 * i, 128 * i + 128)
            at = 4 * u + i
            cell = ce_in[u:u + 1, lanes]
            xce[u, i:i + 1, :] = cell.astype(F32)
            row_i[at:at + 1, :] = (cell // 256) & 15
            col_i[at:at + 1, :] = cell & 255
            state[at:at + 1, :] = ph_in[u:u + 1, lanes]
            state[32 + at:33 + at, :] = en_in[u:u + 1, lanes]
        xce[u, 4:8, :] = jnp.zeros((4, 128), F32)

    def build_onehot():
        iota = lax.broadcasted_iota(jnp.int32, (256, 128), 0)
        for u in range(8):
            for i in range(4):
                at = 4 * u + i
                hot = jnp.where(iota == col_i[at:at + 1, :], 1.0, 0.0)
                onehot[u, :, 128 * i:128 * i + 128] = hot.astype(BF16)

    build_onehot()
    loads[0].wait()
    pl.semaphore_wait(barrier, 95)

    nc = (c + 1) % CUTS
    sure_send(own.at[:, 6:8], halo, s_halo, r_halo, nc, b)
    for u in range(8):
        for k in (1, 2):
            j = (8 * c + u - k + SLOTS) % SLOTS
            dc, db = coords(j, half)
            send(xce.at[u], rxce.at[k - 1, place], s_xce.at[k - 1, u], r_xce.at[k - 1, place], dc, db)

    loads[4].wait()
    loads[5].wait()
    for part in range(2):
        ct = jnp.transpose(colp[part])
        if part == 0:
            places = ((0, 0, 1.0), (1, 1, 1.0))
        else:
            places = ((1, 0, -1.0), (0, 1, 1.0))
        hi, lo = split(ct)
        for kk, nn, sign in places:
            at = (slice(256 * kk, 256 * kk + 256), slice(256 * nn, 256 * nn + 256))
            mh[at] = hi if sign > 0 else -hi
            ml[at] = lo if sign > 0 else -lo
    rows = pl.ds(pl.multiple_of(h * 128, 128), 128)
    for side in range(2):
        cols = pl.ds(pl.multiple_of((h + side - 2 * h * side) * 128, 128), 128)
        rr = split(rowp[0, rows, cols])
        ri = split(rowp[1, rows, cols])
        for n, ref in ((0, ah), (1, al)):
            ref[side, 0:128, 0:128] = rr[n]
            ref[side, 0:128, 128:256] = -ri[n]
            ref[side, 128:256, 0:128] = ri[n]
            ref[side, 128:256, 128:256] = rr[n]

    def sample():
        for u in range(8):
            fu = fld[:, u].reshape(32, 256)
            hi, lo = split(fu)
            got = jnp.dot(jnp.concatenate([hi, lo], axis=0), onehot[u], preferred_element_type=F32)
            got = got[0:32] + got[32:64]
            iota = lax.broadcasted_iota(jnp.int32, (16, 128), 0)
            for i in range(4):
                at = 4 * u + i
                lanes = slice(128 * i, 128 * i + 128)
                mask = iota == row_i[at:at + 1, :]
                for part in range(2):
                    picked = jnp.where(mask, got[16 * part:16 * part + 16, lanes], 0.0)
                    samp[part, at:at + 1, :] = jnp.sum(picked, axis=0, keepdims=True)

    def deposit():
        for u in range(8):
            iota = lax.broadcasted_iota(jnp.int32, (16, 128), 0)
            pieces = []
            for i in range(4):
                at = 4 * u + i
                mask = iota == row_i[at:at + 1, :]
                pieces.append(jnp.concatenate(
                    [jnp.where(mask, emit[n, at:at + 1, :], 0.0).astype(BF16) for n in range(4)], axis=0))
            weights = jnp.concatenate(pieces, axis=1)
            add = lax.dot_general(weights, onehot[u], (((1,), (1,)), ((), ())), preferred_element_type=F32)
            fld[:, u] = fld[:, u] + (add[0:32] + add[32:64]).reshape(2, 16, 256)

    def kick(cosine, sine):
        energy = state[32:64, :] - kick_rate * (samp[0] * cosine - samp[1] * sine)
        phase = state[0:32, :] + energy
        state[0:32, :] = phase
        state[32:64, :] = energy
        cosine, sine = jnp.cos(phase), jnp.sin(phase)
        for n, value in ((0, source_gain * cosine), (1, -source_gain * sine)):
            high = value.astype(BF16).astype(F32)
            emit[n] = high
            emit[2 + n] = value - high
        return cosine, sine

    def add_sums(period, cosine, sine):
        line = lax.broadcasted_iota(jnp.int32, (8, 128), 0)
        total = state[64:72, :]
        total = total + jnp.where(line == 2 * period, jnp.sum(cosine, axis=0, keepdims=True), 0.0)
        total = total + jnp.where(line == 2 * period + 1, -jnp.sum(sine, axis=0, keepdims=True), 0.0)
        state[64:72, :] = total

    def sweep_cols(target, after):
        f = fld[...].reshape(2, 128, 256)
        parts = [split(f[0]), split(f[1])]
        lh = jnp.concatenate([parts[0][0], parts[1][0]], axis=1)
        ll = jnp.concatenate([parts[0][1], parts[1][1]], axis=1)
        for part in range(2):
            lanes = slice(256 * part, 256 * part + 256)
            g = jnp.dot(lh, mh[:, lanes], preferred_element_type=F32)
            g = g + jnp.dot(lh, ml[:, lanes], preferred_element_type=F32)
            g = g + jnp.dot(ll, mh[:, lanes], preferred_element_type=F32)
            target[part] = g.reshape(8, 16, 256)
            after(part)

    def rows_of(side, g):
        hi, lo = split(g)
        out = jnp.dot(ah[side], hi, preferred_element_type=F32)
        out = out + jnp.dot(al[side], hi, preferred_element_type=F32)
        return out + jnp.dot(ah[side], lo, preferred_element_type=F32)

    sure_await(halo, s_halo, r_halo)
    one = shifts[0] == 1
    for u in range(8):
        if u == 0:
            near, far = halo[:, 1], halo[:, 0]
            near = jnp.where(c > 0, near, 0.0)
            far = jnp.where(c > 0, far, 0.0)
        elif u == 1:
            near, far = own[:, 0], jnp.where(c > 0, halo[:, 1], 0.0)
        else:
            near, far = own[:, u - 1], own[:, u - 2]
        fld[:, u] = jnp.where(one, near, far)
    sample()
    kick(jnp.cos(state[0:32, :]), jnp.sin(state[0:32, :]))
    for u in range(8):
        xst[u, 0:4, :] = state[4 * u:4 * u + 4, :]
        xst[u, 4:8, :] = state[32 + 4 * u:36 + 4 * u, :]
    for u in range(8):
        for k in (1, 2):
            j = (8 * c + u - k + SLOTS) % SLOTS
            dc, db = coords(j, half)
            send(xst.at[u], rxst.at[k - 1, place], s_xst.at[k - 1, u], r_xst.at[k - 1, place], dc, db)
    deposit()
    sweep_cols(gx, lambda part: None)
    for u in range(8):
        send(gx.at[:, u], gown.at[0, :, place], s_a2a.at[u], r_a2a.at[place], z * 2 + half, 8 * h + u)

    partner = c + 1 - 2 * h
    for v in range(8):
        await_from(gown.at[0, :, v], s_a2a.at[v], r_a2a.at[v], z * 2 + half, 8 * h + v)
        sure_send(gown.at[0, :, v], goth.at[0, :, v], s_fwd.at[v], r_fwd.at[v], partner, b)
    acc = rows_of(0, gown[0].reshape(256, 256))
    for v in range(8):
        sure_await(goth.at[0, :, v], s_fwd.at[v], r_fwd.at[v])
    acc = acc + rows_of(1, goth[0].reshape(256, 256))

    moved = 0
    for period in range(1, 4):
        one = shifts[period] == 1
        moved = moved + shifts[period]
        fresh = ((slot + moved) & 255) < shifts[period]
        fld[...] = jnp.where(fresh, 0.0, acc).reshape(2, 8, 16, 256)
        if period == 1:
            for k in (1, 2):
                for v in range(8):
                    j = (slot + k) % SLOTS
                    dc, db = j // 8, 8 * h + v
                    await_from(rxce.at[k - 1, v], s_xce.at[k - 1, v], r_xce.at[k - 1, v], dc, db)
                    await_from(rxst.at[k - 1, v], s_xst.at[k - 1, v], r_xst.at[k - 1, v], dc, db)
            for v in range(8):
                tile = jnp.where(one, rxst[0, v], rxst[1, v])
                state[4 * v:4 * v + 4, :] = tile[0:4]
                state[32 + 4 * v:36 + 4 * v, :] = tile[4:8]
                cell_f[0, 4 * v:4 * v + 4, :] = jnp.where(one, rxce[0, v], rxce[1, v])[0:4]
            state[64:72, :] = jnp.zeros((8, 128), F32)
        else:
            for k in (1, 2):
                sure_await(rce.at[period - 2, k - 1], s_ce.at[period - 2, k - 1], r_ce.at[period - 2, k - 1])
                sure_await(rst.at[period - 2, k - 1], s_st.at[period - 2, k - 1], r_st.at[period - 2, k - 1])
            state[...] = jnp.where(one, rst[period - 2, 0], rst[period - 2, 1])
            cell_f[period - 1] = jnp.where(one, rce[period - 2, 0], rce[period - 2, 1])
        if period < 3:
            for k in (1, 2):
                dc, db = coords((slot - k + SLOTS) % SLOTS, h)
                sure_send(cell_f.at[period - 1], rce.at[period - 1, k - 1],
                          s_ce.at[period - 1, k - 1], r_ce.at[period - 1, k - 1], dc, db)
        cell = cell_f[period - 1].astype(jnp.int32)
        row_i[...] = (cell // 256) & 15
        col_i[...] = cell & 255
        build_onehot()
        sample()
        cosine, sine = jnp.cos(state[0:32, :]), jnp.sin(state[0:32, :])
        add_sums(period - 1, cosine, sine)
        cosine, sine = kick(cosine, sine)
        if period < 3:
            efin_at = period - 1
            efin[efin_at] = state[...]
            for k in (1, 2):
                dc, db = coords((slot - k + SLOTS) % SLOTS, h)
                sure_send(efin.at[efin_at], rst.at[period - 1, k - 1],
                          s_st.at[period - 1, k - 1], r_st.at[period - 1, k - 1], dc, db)
        else:
            add_sums(3, cosine, sine)
            efin[2] = state[...]
            for v in range(8):
                xst2 = jnp.concatenate([state[4 * v:4 * v + 4, :], state[32 + 4 * v:36 + 4 * v, :]], axis=0)
                efin[3, 8 * v:8 * v + 8, :] = xst2
            c1, c2 = (slot + 3) // 8, (slot + 6) // 8
            for n, cc in ((0, c1), (1, c2)):
                extra = None if n == 0 else c1 != c2
                w = slot - 8 * cc + 6
                dc = cc % CUTS
                for v in range(8):
                    send(efin.at[3, 8 * v:8 * v + 8], rel.at[w], s_el.at[n, v], r_el.at[w], dc, 8 * h + v, extra)
                for v in range(16):
                    send(efin.at[2, 64:72], rsum.at[w, h], s_sum.at[n, v], r_sum.at[w, h], dc, v, extra)
        deposit()

        def exchange(part, period=period):
            sure_send(gown.at[period, part], goth.at[period, part],
                      s_ex.at[period - 1, part], r_ex.at[period - 1, part], partner, b)

        sweep_cols(gown.at[period], exchange)
        acc = rows_of(0, gown[period].reshape(256, 256))
        for part in range(2):
            sure_await(goth.at[period, part], s_ex.at[period - 1, part], r_ex.at[period - 1, part])
        acc = acc + rows_of(1, goth[period].reshape(256, 256))

    fin[...] = acc.reshape(2, 8, 16, 256)
    c1, c2 = (slot + 3) // 8, (slot + 6) // 8
    for n, cc in ((0, c1), (1, c2)):
        extra = None if n == 0 else c1 != c2
        w = slot - 8 * cc + 6
        dc = cc % CUTS
        for v in range(8):
            send(fin.at[:, v], rfld.at[w], s_fld.at[n, v], r_fld.at[w], dc, 8 * h + v, extra)

    for w in range(11):
        j = (8 * c - 6 + w + SLOTS) % SLOTS
        for core in range(2):
            dc, db = coords(j, core)
            await_from(rsum.at[w, core], s_sum.at[0, 0], r_sum.at[w, core], dc, db)
        dc, db = coords(j, half)
        await_from(rel.at[w], s_el.at[0, 0], r_el.at[w], dc, db)
    base = jnp.clip(6 - moved, 0, 3)
    lane = lax.broadcasted_iota(jnp.int32, (8, 8), 1)
    sums = jnp.zeros((8, 8), F32)
    for u in range(8):
        tile = rel[base + u]
        for i in range(4):
            lanes = slice(128 * i, 128 * i + 128)
            phase_out[u:u + 1, lanes] = tile[i:i + 1]
            energy_out[u:u + 1, lanes] = tile[4 + i:5 + i]
        pair = rsum[base + u]
        total = jnp.sum(pair[0] + pair[1], axis=1, keepdims=True)
        sums = jnp.where(lane == u, total, sums)
    sums_out[...] = sums * ELEC ** (-0.5)
    for w in range(11):
        j = (8 * c - 6 + w + SLOTS) % SLOTS
        dc, db = coords(j, half)
        await_from(rfld.at[w], s_fld.at[0, 0], r_fld.at[w], dc, db)
    for u in range(8):
        field_out[:, u] = rfld[base + u]

    for there, src, dst, ss, rs in sends:
        copy = remote(src, dst, ss, rs, c, b)
        if there is None:
            copy.wait_send()
        else:
            @pl.when(there)
            def _():
                copy.wait_send()


def shards(field, row_prop, col_prop, phase, energy, cells, shifts):
    V = pltpu.VMEM
    D = pltpu.SemaphoreType.DMA
    blocks = (2, 8, 16, 256)
    scratch = [
        V(blocks, F32), V((2, 2, 16, 256), F32), V((2, 256, 256), F32), V((2, 256, 256), F32),
        V((8, 512), F32), V((8, 512), F32), V((8, 512), jnp.int32),
        V((512, 512), BF16), V((512, 512), BF16), V((2, 256, 256), BF16), V((2, 256, 256), BF16),
        V((3, 32, 128), F32), V((32, 128), jnp.int32), V((32, 128), jnp.int32),
        V((8, 256, 512), BF16), V(blocks, F32), V(blocks, F32), V((4, *blocks), F32), V((4, *blocks), F32),
        V((2, 32, 128), F32), V((4, 32, 128), F32), V((72, 128), F32),
        V((8, 8, 128), F32), V((8, 8, 128), F32), V((2, 8, 8, 128), F32), V((2, 8, 8, 128), F32),
        V((2, 2, 72, 128), F32), V((2, 2, 32, 128), F32), V((4, 72, 128), F32),
        V(blocks, F32), V((11, 2, 16, 256), F32), V((11, 8, 128), F32), V((11, 2, 8, 128), F32),
        D((6,)), D, D, D((8,)), D((8,)), D((8,)), D((8,)), D((3, 2)), D((3, 2)),
        D((2, 8)), D((2, 8)), D((2, 8)), D((2, 8)), D((2, 2)), D((2, 2)), D((2, 2)), D((2, 2)),
        D((2, 8)), D((11,)), D((2, 8)), D((11,)), D((2, 16)), D((11, 2)),
    ]
    hbm = pl.BlockSpec(memory_space=pl.ANY)
    vmem = pl.BlockSpec(memory_space=pltpu.VMEM)
    out = pl.pallas_call(
        kernel,
        out_shape=(jax.ShapeDtypeStruct(blocks, F32), jax.ShapeDtypeStruct((8, 512), F32),
                   jax.ShapeDtypeStruct((8, 512), F32), jax.ShapeDtypeStruct((8, 8), F32)),
        in_specs=[pl.BlockSpec(memory_space=pltpu.SMEM)] + [hbm] * 6,
        out_specs=(vmem, vmem, vmem, vmem),
        scratch_shapes=scratch,
        compiler_params=pltpu.CompilerParams(
            collective_id=0, has_side_effects=True, vmem_limit_bytes=48 << 20),
    )(shifts, field, row_prop, col_prop, phase, energy, cells)
    return out[0], out[1], out[2], out[3].reshape(4, 2, 8)


def solution(mesh):
    return jax.shard_map(
        shards,
        mesh=mesh,
        in_specs=(
            P(None, "cuts", "row", None),
            P(),
            P(),
            P("cuts", "row"),
            P("cuts", "row"),
            P("cuts", "row"),
            P(),
        ),
        out_specs=(
            P(None, "cuts", "row", None),
            P("cuts", "row"),
            P("cuts", "row"),
            P(None, None, "cuts"),
        ),
        check_vma=False,
    )
```

profile of v0, /device:TPU:14, one launch (start us, length us, event | category | flops | bytes accessed | tf_op | source)
XLA Modules:
  0.0 65.2 jit_solution(13036691873658386907)
XLA Ops:
  0.6 0.0 copy-start
  0.6 1.0 %copy-done = f32[2,256,256]{2,1,0:T(8,128)S(1)} copy-done((f32[2,256,256]{2,1,0:T(8,128)S(1)}, f32[2,256,256]{2,1,0:T(8,128)}, u32[]{:S(2)}) %copy-start) | copy-done | bytes 524312
  1.7 0.0 copy-start.1
  1.7 1.0 %copy-done.1 = f32[2,256,256]{2,1,0:T(8,128)S(1)} copy-done((f32[2,256,256]{2,1,0:T(8,128)S(1)}, f32[2,256,256]{2,1,0:T(8,128)}, u32[]{:S(2)}) %copy-start.1) | copy-done | bytes 524312
  2.7 0.0 copy-start.2
  2.7 0.9 %copy-done.2 = f32[2,8,16,256]{3,2,1,0:T(8,128)S(1)} copy-done((f32[2,8,16,256]{3,2,1,0:T(8,128)S(1)}, f32[2,8,16,256]{3,2,1,0:T(8,128)}, u32[]{:S(2)}) %copy-start.2) | copy-done | bytes 262168
  3.7 0.0 copy-start.3
  3.7 0.7 %copy-done.3 = f32[8,512]{1,0:T(8,128)S(1)} copy-done((f32[8,512]{1,0:T(8,128)S(1)}, f32[8,512]{1,0:T(8,128)}, u32[]{:S(2)}) %copy-start.3) | copy-done | bytes 16408
  4.4 0.0 copy-start.4
  4.4 0.7 %copy-done.4 = f32[8,512]{1,0:T(8,128)S(1)} copy-done((f32[8,512]{1,0:T(8,128)S(1)}, f32[8,512]{1,0:T(8,128)}, u32[]{:S(2)}) %copy-start.4) | copy-done | bytes 16408
  5.1 0.0 copy-start.5
  5.1 0.7 %copy-done.5 = s32[8,512]{1,0:T(8,128)S(1)} copy-done((s32[8,512]{1,0:T(8,128)S(1)}, s32[8,512]{1,0:T(8,128)}, u32[]{:S(2)}) %copy-start.5) | copy-done | bytes 16408
  5.8 0.0 copy-start.6
  5.8 0.7 %copy-done.6 = s32[4]{0:T(128)S(1)} copy-done((s32[4]{0:T(128)S(1)}, s32[4]{0:T(128)}, u32[]{:S(2)}) %copy-start.6) | copy-done | bytes 40
  6.5 56.2 %shard_map.102 = (f32[2,8,16,256]{3,2,1,0:T(8,128)S(1)}, f32[8,512]{1,0:T(8,128)S(1)}, f32[8,512]{1,0:T(8,128)S(1)}, f32[8,8]{1,0:T(8,128)S(1)}) custom-call(s32[4]{0:T(128)S(1)} %copy-done.6, f32[2,8,16,256]{3,2,1,0:T(8,128)S(1)} %copy-done.2, f32[2,256,256]{2,1,0:T(8,128)S(1)} %copy-done, f32[2,256,256]{2,1,0:T(8,128)S(1)} %copy-done.1, ...), custom_call_target="tpu_custom_call" | custom-call | tf_op jit(solution)/shard_map/pallas_call | solution.py:394
  62.6 0.7 %copy.15 = f32[2,8,16,256]{3,2,1,0:T(8,128)} copy(f32[2,8,16,256]{3,2,1,0:T(8,128)S(1)} %get-tuple-element.16) | data formatting | bytes 524288
  63.4 0.6 copy.16
  64.0 0.6 copy.17
  64.6 0.6 copy.18
Async XLA Ops:
  0.6 1.0 %copy-start = (f32[2,256,256]{2,1,0:T(8,128)S(1)}, f32[2,256,256]{2,1,0:T(8,128)}, u32[]{:S(2)}) copy-start(f32[2,256,256]{2,1,0:T(8,128)} %row_in.1) | copy-start | bytes 1572868
  1.7 1.0 %copy-start.1 = (f32[2,256,256]{2,1,0:T(8,128)S(1)}, f32[2,256,256]{2,1,0:T(8,128)}, u32[]{:S(2)}) copy-start(f32[2,256,256]{2,1,0:T(8,128)} %col_in.1) | copy-start | bytes 1572868
  2.7 0.9 %copy-start.2 = (f32[2,8,16,256]{3,2,1,0:T(8,128)S(1)}, f32[2,8,16,256]{3,2,1,0:T(8,128)}, u32[]{:S(2)}) copy-start(f32[2,8,16,256]{3,2,1,0:T(8,128)} %field_in.1) | copy-start | bytes 786436
  3.7 0.7 %copy-start.3 = (f32[8,512]{1,0:T(8,128)S(1)}, f32[8,512]{1,0:T(8,128)}, u32[]{:S(2)}) copy-start(f32[8,512]{1,0:T(8,128)} %phase_in.1) | copy-start | bytes 49156
  4.4 0.7 %copy-start.4 = (f32[8,512]{1,0:T(8,128)S(1)}, f32[8,512]{1,0:T(8,128)}, u32[]{:S(2)}) copy-start(f32[8,512]{1,0:T(8,128)} %energy_in.1) | copy-start | bytes 49156
  5.1 0.7 %copy-start.5 = (s32[8,512]{1,0:T(8,128)S(1)}, s32[8,512]{1,0:T(8,128)}, u32[]{:S(2)}) copy-start(s32[8,512]{1,0:T(8,128)} %cells_in.1) | copy-start | bytes 49156
  5.8 0.7 %copy-start.6 = (s32[4]{0:T(128)S(1)}, s32[4]{0:T(128)}, u32[]{:S(2)}) copy-start(s32[4]{0:T(128)} %shifts.1) | copy-start | bytes 52
where the time goes:
time: 65.6 us; the launch traced here: 65.2 us
  Pallas kernels  56.2 us (86%)
  local copies, waits for them, and re-layouts  8.34 us (13%)
  between operations  0.66 us (1%)
    pallas_call x1, Pallas kernels, shards(): pl.pallas_call(kernel, out_shape=(jax.ShapeDtypeStruct(blocks, F32), jax....  56.2 us
    unnamed x18, local copies, waits for them, and re-layouts  8.34 us

commit v1 on v0

v1 whole, which is shorter than its diff:
```python
import jax
import jax.numpy as jnp
from jax import lax
from jax.experimental import pallas as pl
from jax.experimental.pallas import tpu as pltpu
from jax.sharding import PartitionSpec as P

F32 = jnp.float32
BF16 = jnp.bfloat16
MESH = pl.DeviceIdType.MESH
ELEC = 8192
CUTS = 32
SLOTS = 256
VMEM_LIMIT = 67_000_000
kick_rate = 0.5
source_gain = 0.5


def split(x):
    high = x.astype(BF16)
    return high, (x - high.astype(F32)).astype(BF16)


PATH = (0, 1, 5, 6, 10, 11, 15, 12, 8, 4, 7, 3, 2, 14, 13, 9)


def lookup(table, i):
    low = sum(n << (3 * (q % 8)) for q, n in enumerate(t % 8 for t in table[:8]))
    high = sum(n << (3 * (q % 8)) for q, n in enumerate(t % 8 for t in table[8:]))
    tops = sum((t // 8) << q for q, t in enumerate(table))
    word = jnp.where(i < 8, low, high)
    return ((word >> (3 * (i % 8))) & 7) + 8 * ((tops >> i) & 1)


def chip_of(j):
    z, at = j // 16, lookup(PATH, j % 16)
    return z, (at % 4 + z) % 4 + 4 * ((at // 4 + 2 * z) % 4)


def slot_of(z, b):
    at = (b % 4 + 3 * z) % 4 + 4 * ((b // 4 + 2 * z) % 4)
    return z * 16 + lookup(tuple(PATH.index(q) for q in range(16)), at)


def kernel(shifts_in, field_in, row_in, col_in, phase_in, energy_in, cells_in,
           field_out, phase_out, energy_out, sums_out,
           own, rowp, colp, ph_in, en_in, ce_in, mh, ml, ah, al,
           key_i, col_f, onehot, fld, arr, gown, goth, samp, emit, state, cell_f,
           shifts, out_sums, out_ph, out_en, out_fld, xel, rxel, sst, rst, rce, psum, psum_in, efin, fin, rfld, rel,
           lsem, s_a2a, r_a2a, s_xel, r_xel, s_ex, r_ex, s_st, r_st, s_ce, r_ce,
           s_ps, r_ps, s_fld, r_fld, s_el, r_el):
    c = lax.axis_index("cuts")
    b = lax.axis_index("row")
    z = c // 2
    h = c % 2
    half = b // 8
    place = b % 8
    slot = slot_of(z, b)
    group = (slot // 8) % 2
    base_cut = slot // 8
    partner = c + 1 - 2 * h
    sends = []
    scope = []

    def mark(name):
        if scope:
            scope.pop().__exit__(None, None, None)
        if name:
            scope.append(jax.named_scope(name))
            scope[0].__enter__()

    def remote(src, dst, ss, rs, dc, db):
        return pltpu.make_async_remote_copy(
            src_ref=src, dst_ref=dst, send_sem=ss, recv_sem=rs,
            device_id=(dc, db), device_id_type=MESH)

    def send(src, dst, ss, rs, dc, db, extra=None):
        here = (dc == c) & (db == b)
        there = jnp.logical_not(here)
        if extra is not None:
            here = here & extra
            there = there & extra

        @pl.when(there)
        def _():
            remote(src, dst, ss, rs, dc, db).start()

        @pl.when(here)
        def _():
            dst[...] = src[...]

        sends.append((there, src, dst, ss, rs))

    def sure_send(src, dst, ss, rs, dc, db):
        remote(src, dst, ss, rs, dc, db).start()
        sends.append((None, src, dst, ss, rs))

    def await_from(dst, ss, rs, dc, db):
        @pl.when(jnp.logical_not((dc == c) & (db == b)))
        def _():
            remote(dst, dst, ss, rs, dc, db).wait_recv()

    def sure_await(dst, ss, rs):
        remote(dst, dst, ss, rs, c, b).wait_recv()

    mark("start")
    loads = [(phase_in, ph_in), (energy_in, en_in), (cells_in, ce_in), (field_in, own),
             (col_in, colp), (row_in, rowp), (shifts_in, shifts)]
    loads = [pltpu.make_async_copy(src, dst, lsem.at[n]) for n, (src, dst) in enumerate(loads)]
    for copy in loads:
        copy.start()

    barrier = pltpu.get_barrier_semaphore()
    below = (base_cut + 1) % CUTS
    itself = (half == h) & ((base_cut == c) | ((below == c) & (slot % 8 >= 6)))
    def greet(dc, extra=None):
        for v in range(8):
            ok = jnp.logical_not((dc == c) & (8 * h + v == b))

            @pl.when(ok if extra is None else ok & extra)
            def _():
                pl.semaphore_signal(barrier, inc=1, device_id=(dc, 8 * h + v), device_id_type=MESH)

    greet(base_cut)
    greet(below, slot % 8 >= 6)
    for k in (1, 2):
        pz, pb = chip_of((slot + k) % SLOTS)
        pl.semaphore_signal(barrier, inc=1, device_id=(pz * 2 + h, pb), device_id_type=MESH)
    pl.semaphore_signal(barrier, inc=1, device_id=(partner, b), device_id_type=MESH)
    pl.semaphore_signal(barrier, inc=1, device_id=((c + CUTS - 1) % CUTS, b), device_id_type=MESH)

    mark("unpack")
    for n in (0, 1, 2):
        loads[n].wait()
    for u in range(8):
        for i in range(4):
            lanes = slice(128 * i, 128 * i + 128)
            xel[u, i:i + 1, :] = ph_in[u:u + 1, lanes]
            xel[u, 4 + i:5 + i, :] = en_in[u:u + 1, lanes]
            xel[u, 8 + i:9 + i, :] = ce_in[u:u + 1, lanes].astype(F32)
        xel[u, 12:16, :] = jnp.zeros((4, 128), F32)

    mark("w_barrier")
    loads[3].wait()
    pl.semaphore_wait(barrier, 14 - jnp.where(itself, 1, 0))

    mark("send0")
    for i in range(8):
        u = (place + i) % 8
        for k in (1, 2):
            pz, pb = chip_of((8 * c + u - k + SLOTS) % SLOTS)
            send(xel.at[u], rxel.at[k - 1, place], s_xel.at[k - 1, u], r_xel.at[k - 1, place], pz * 2 + half, pb)
    for i in range(8):
        u = (place + i) % 8
        _, db = chip_of(8 * c + u)
        send(own.at[:, u], arr.at[:, place], s_a2a.at[u], r_a2a.at[place], z * 2 + half, db)

    mark("prep")
    loads[4].wait()
    loads[5].wait()
    for part in range(2):
        hi, lo = split(jnp.transpose(colp[part]))
        places = ((0, 0, 1), (1, 1, 1)) if part == 0 else ((1, 0, -1), (0, 1, 1))
        for kk, nn, sign in places:
            at = (slice(256 * kk, 256 * kk + 256), slice(256 * nn, 256 * nn + 256))
            mh[at] = hi if sign > 0 else -hi
            ml[at] = lo if sign > 0 else -lo
    rows = pl.ds(pl.multiple_of(h * 128, 128), 128)
    for side in range(2):
        cols = pl.ds(pl.multiple_of((h + side - 2 * h * side) * 128, 128), 128)
        rr = split(rowp[0, rows, cols])
        ri = split(rowp[1, rows, cols])
        for n, ref in ((0, ah), (1, al)):
            ref[side, 0:128, 0:128] = rr[n]
            ref[side, 0:128, 128:256] = -ri[n]
            ref[side, 128:256, 0:128] = ri[n]
            ref[side, 128:256, 128:256] = rr[n]

    def build_onehot(period):
        if period < 3:
            relay(cell_f.at[period], rce, s_ce, r_ce, period)
        cell = cell_f[period].astype(jnp.int32)
        key_i[...] = ((cell >> 8) & 15) + ((cell >> 7) & 1) * 16
        col_f[...] = (cell & 127).astype(F32)
        iota = lax.broadcasted_iota(jnp.int32, (128, 128), 0).astype(F32).astype(BF16)
        for u in range(8):
            for i in range(4):
                at = 4 * u + i
                col = jnp.broadcast_to(col_f[at:at + 1, :], (128, 128)).astype(BF16)
                onehot[u, :, 128 * i:128 * i + 128] = jnp.where(iota == col, 1.0, 0.0).astype(BF16)

    def relay(src, dst, ss, rs, period):
        for k in (1, 2):
            pz, pb = chip_of((slot - k + SLOTS) % SLOTS)
            sure_send(src, dst.at[period, k - 1], ss.at[period, k - 1], rs.at[period, k - 1], pz * 2 + h, pb)

    def sample():
        iota = lax.broadcasted_iota(jnp.int32, (32, 128), 0)
        for u in range(8):
            fu = jnp.concatenate([fld[p, u, :, 128 * q:128 * q + 128] for p in range(2) for q in range(2)], axis=0)
            hi, lo = split(fu)
            got = jnp.dot(jnp.concatenate([hi, lo], axis=0), onehot[u], preferred_element_type=F32)
            got = got[0:64] + got[64:128]
            for i in range(4):
                at = 4 * u + i
                lanes = slice(128 * i, 128 * i + 128)
                mask = iota == key_i[at:at + 1, :]
                for part in range(2):
                    picked = jnp.where(mask, got[32 * part:32 * part + 32, lanes], 0.0)
                    samp[part, at:at + 1, :] = jnp.sum(picked, axis=0, keepdims=True)

    def deposit():
        iota = lax.broadcasted_iota(jnp.int32, (32, 128), 0)
        for u in range(8):
            pieces = []
            for i in range(4):
                at = 4 * u + i
                mask = iota == key_i[at:at + 1, :]
                pieces.append(jnp.concatenate(
                    [jnp.where(mask, emit[n, at:at + 1, :], 0.0).astype(BF16) for n in range(4)], axis=0))
            weights = jnp.concatenate(pieces, axis=1)
            add = lax.dot_general(weights, onehot[u], (((1,), (1,)), ((), ())), preferred_element_type=F32)
            add = add[0:64] + add[64:128]
            for p in range(2):
                for q in range(2):
                    lanes = slice(128 * q, 128 * q + 128)
                    rows = slice(32 * p + 16 * q, 32 * p + 16 * q + 16)
                    fld[p, u, :, lanes] = fld[p, u, :, lanes] + add[rows]

    def kick(period):
        cosine, sine = jnp.cos(state[0:32, :]), jnp.sin(state[0:32, :])
        energy = state[32:64, :] - kick_rate * (samp[0] * cosine - samp[1] * sine)
        phase = state[0:32, :] + energy
        cosine, sine = jnp.cos(phase), jnp.sin(phase)
        line = lax.broadcasted_iota(jnp.int32, (8, 128), 0)
        total = state[64:72, :]
        total = total + jnp.where(line == 2 * period, jnp.sum(cosine, axis=0, keepdims=True), 0.0)
        total = total + jnp.where(line == 2 * period + 1, -jnp.sum(sine, axis=0, keepdims=True), 0.0)
        for n, value in ((0, source_gain * cosine), (1, -source_gain * sine)):
            high = value.astype(BF16).astype(F32)
            emit[n] = high
            emit[2 + n] = value - high
        return phase, energy, total

    def sweep_cols(target):
        f = fld[...].reshape(2, 128, 256)
        parts = [split(f[0]), split(f[1])]
        lh = jnp.concatenate([parts[0][0], parts[1][0]], axis=1)
        ll = jnp.concatenate([parts[0][1], parts[1][1]], axis=1)
        for part in range(2):
            lanes = slice(256 * part, 256 * part + 256)
            g = jnp.dot(lh, mh[:, lanes], preferred_element_type=F32)
            g = g + jnp.dot(lh, ml[:, lanes], preferred_element_type=F32)
            g = g + jnp.dot(ll, mh[:, lanes], preferred_element_type=F32)
            target[part] = g.reshape(8, 16, 256)

    def rows_of(side, g):
        hi, lo = split(g)
        out = jnp.dot(ah[side], hi, preferred_element_type=F32)
        out = out + jnp.dot(al[side], hi, preferred_element_type=F32)
        return out + jnp.dot(ah[side], lo, preferred_element_type=F32)

    def to_rows(source, dst, ss, rs):
        c1, c2 = (slot + 5) // 8, (slot + 8) // 8
        for i in range(8):
            v = (place + i) % 8
            for n, cc in ((0, c1), (1, c2)):
                extra = None if n == 0 else c1 != c2
                w = slot - 8 * cc + 8
                send(source(v), dst.at[w], ss.at[n, v], rs.at[w], cc % CUTS, 8 * h + v, extra)

    def cells_for(period):
        mark("w_ce")
        for k in (1, 2):
            sure_await(rce.at[period - 1, k - 1], s_ce.at[period - 1, k - 1], r_ce.at[period - 1, k - 1])
        mark("hot")
        cell_f[period] = jnp.where(shifts[period] == 1, rce[period - 1, 0], rce[period - 1, 1])
        build_onehot(period)

    mark("w_xel")
    for k in (1, 2):
        for v in range(8):
            await_from(rxel.at[k - 1, v], s_xel.at[k - 1, v], r_xel.at[k - 1, v],
                       ((slot + k) % SLOTS) // 8, 8 * h + v)
    loads[6].wait()
    mark("first")
    one = shifts[0] == 1
    for v in range(8):
        tile = jnp.where(one, rxel[0, v], rxel[1, v])
        state[4 * v:4 * v + 4, :] = tile[0:4]
        state[32 + 4 * v:36 + 4 * v, :] = tile[4:8]
        cell_f[0, 4 * v:4 * v + 4, :] = tile[8:12]
    state[64:72, :] = jnp.zeros((8, 128), F32)
    build_onehot(0)
    moved = 0
    acc = None
    for period in range(4):
        one = shifts[period] == 1
        moved = moved + shifts[period]
        fresh = ((slot + moved) & 255) < shifts[period]
        if period > 0:
            mark("w_st")
            for k in (1, 2):
                sure_await(rst.at[period - 1, k - 1], s_st.at[period - 1, k - 1], r_st.at[period - 1, k - 1])
            state[...] = jnp.where(one, rst[period - 1, 0], rst[period - 1, 1])
        if period == 0:
            mark("w_a2a")
            for v in range(8):
                await_from(arr.at[:, v], s_a2a.at[v], r_a2a.at[v], z * 2 + group, 8 * h + v)
            fld[...] = jnp.where(fresh, 0.0, arr[...])
        else:
            fld[...] = jnp.where(fresh, 0.0, acc).reshape(2, 8, 16, 256)
        mark("samp")
        sample()
        mark("kick")
        phase, energy, total = kick(period)
        if period < 3:
            sst[period, 0:32, :] = phase
            sst[period, 32:64, :] = energy
            sst[period, 64:72, :] = total
            relay(sst.at[period], rst, s_st, r_st, period)
        else:
            state[0:32, :] = phase
            state[32:64, :] = energy
            psum[...] = total
            sure_send(psum, psum_in, s_ps, r_ps, partner, b)
        mark("dep")
        deposit()

        mark("col")
        sweep_cols(gown.at[period])
        for part in range(2):
            sure_send(gown.at[period, part], goth.at[period, part],
                      s_ex.at[period, part], r_ex.at[period, part], partner, b)
        mark("rowown")
        acc = rows_of(0, gown[period].reshape(256, 256))
        if period < 3:
            cells_for(period + 1)
        else:
            mark("elsend")
            sure_await(psum_in, s_ps, r_ps)
            total = psum[...] + psum_in[...]
            for v in range(8):
                efin[v, 0:4, :] = state[4 * v:4 * v + 4, :]
                efin[v, 4:8, :] = state[32 + 4 * v:36 + 4 * v, :]
                efin[v, 8:16, :] = total
            to_rows(lambda v: efin.at[v], rel, s_el, r_el)
        mark("w_ex")
        for part in range(2):
            sure_await(goth.at[period, part], s_ex.at[period, part], r_ex.at[period, part])
        mark("rowoth")
        acc = acc + rows_of(1, goth[period].reshape(256, 256))

    mark("fsend")
    fin[...] = acc.reshape(2, 8, 16, 256)
    to_rows(lambda v: fin.at[:, v], rfld, s_fld, r_fld)

    mark("w_small")
    for w in range(11):
        j = (8 * c - 8 + w + SLOTS) % SLOTS
        pz, pb = chip_of(j)
        await_from(rel.at[w], s_el.at[0, 0], r_el.at[w], pz * 2 + half, pb)
    mark("smallout")
    base = jnp.clip(8 - moved, 0, 3)
    lane = lax.broadcasted_iota(jnp.int32, (8, 8), 1)
    sums = jnp.zeros((8, 8), F32)
    for u in range(8):
        tile = rel[base + u]
        for i in range(4):
            lanes = slice(128 * i, 128 * i + 128)
            out_ph[u:u + 1, lanes] = tile[i:i + 1]
            out_en[u:u + 1, lanes] = tile[4 + i:5 + i]
        sums = jnp.where(lane == u, jnp.sum(tile[8:16], axis=1, keepdims=True), sums)
    out_sums[...] = sums * ELEC ** (-0.5)
    stores = [(out_ph, phase_out), (out_en, energy_out), (out_sums, sums_out), (out_fld, field_out)]
    stores = [pltpu.make_async_copy(src, dst, lsem.at[7 + n]) for n, (src, dst) in enumerate(stores)]
    for copy in stores[:3]:
        copy.start()
    mark("w_fld")
    for w in range(11):
        j = (8 * c - 8 + w + SLOTS) % SLOTS
        pz, pb = chip_of(j)
        await_from(rfld.at[w], s_fld.at[0, 0], r_fld.at[w], pz * 2 + half, pb)
    mark("fout")
    for u in range(8):
        out_fld[:, u] = rfld[base + u]
    stores[3].start()

    mark("drain")
    for there, src, dst, ss, rs in sends:
        copy = remote(src, dst, ss, rs, c, b)
        if there is None:
            copy.wait_send()
        else:
            @pl.when(there)
            def _():
                copy.wait_send()
    for copy in stores:
        copy.wait()
    mark(None)


def hand_over(field, phase, energy, sums, field_out, phase_out, energy_out, bunching_out,
              a, p, e, q, out, sem):
    ins = [(field, a), (phase, p), (energy, e), (sums, q)]
    outs = [(a, field_out), (p, phase_out), (e, energy_out), (out, bunching_out)]
    ins = [pltpu.make_async_copy(src, dst, sem.at[n]) for n, (src, dst) in enumerate(ins)]
    outs = [pltpu.make_async_copy(src, dst, sem.at[4 + n]) for n, (src, dst) in enumerate(outs)]
    for copy in ins:
        copy.start()
    for n in (3, 1, 2, 0):
        ins[n].wait()
        if n == 3:
            for period in range(4):
                out[period] = q[2 * period:2 * period + 2]
        outs[n].start()
    for copy in outs:
        copy.wait()


def shards(field, row_prop, col_prop, phase, energy, cells, shifts):
    V = pltpu.VMEM
    D = pltpu.SemaphoreType.DMA
    blocks = (2, 8, 16, 256)
    square = (2, 256, 256)
    scratch = [
        V(blocks, F32), V(square, F32), V(square, F32),
        V((8, 512), F32), V((8, 512), F32), V((8, 512), jnp.int32),
        V((512, 512), BF16), V((512, 512), BF16), V(square, BF16), V(square, BF16),
        V((32, 128), jnp.int32), V((32, 128), F32), V((8, 128, 512), BF16),
        V(blocks, F32), V(blocks, F32), V((4, *blocks), F32), V((4, *blocks), F32),
        V((2, 32, 128), F32), V((4, 32, 128), F32), V((72, 128), F32), V((4, 32, 128), F32),
        pltpu.SMEM((4,), jnp.int32), V((8, 8), F32), V((8, 512), F32), V((8, 512), F32), V(blocks, F32),
        V((8, 16, 128), F32), V((2, 8, 16, 128), F32), V((3, 72, 128), F32),
        V((3, 2, 72, 128), F32), V((3, 2, 32, 128), F32), V((8, 128), F32), V((8, 128), F32),
        V((8, 16, 128), F32), V(blocks, F32), V((11, 2, 16, 256), F32), V((11, 16, 128), F32),
        D((11,)), D((8,)), D((8,)), D((2, 8)), D((2, 8)), D((4, 2)), D((4, 2)),
        D((3, 2)), D((3, 2)), D((3, 2)), D((3, 2)), D, D,
        D((2, 8)), D((11,)), D((2, 8)), D((11,)),
    ]
    hbm = pl.BlockSpec(memory_space=pl.ANY)
    results = (jax.ShapeDtypeStruct(blocks, F32), jax.ShapeDtypeStruct((8, 512), F32),
               jax.ShapeDtypeStruct((8, 512), F32))
    out = pl.pallas_call(
        kernel,
        out_shape=(*results, jax.ShapeDtypeStruct((8, 8), F32)),
        in_specs=[hbm] * 7,
        out_specs=[hbm] * 4,
        scratch_shapes=scratch,
        compiler_params=pltpu.CompilerParams(
            collective_id=0, has_side_effects=True, vmem_limit_bytes=VMEM_LIMIT),
    )(shifts, field, row_prop, col_prop, phase, energy, cells)
    return pl.pallas_call(
        hand_over,
        out_shape=(*results, jax.ShapeDtypeStruct((4, 2, 8), F32)),
        in_specs=[hbm] * 4,
        out_specs=[hbm] * 4,
        scratch_shapes=[V(blocks, F32), V((8, 512), F32), V((8, 512), F32), V((8, 8), F32),
                        V((4, 2, 8), F32), D((8,))],
        compiler_params=pltpu.CompilerParams(vmem_limit_bytes=VMEM_LIMIT),
    )(*out)


def solution(mesh):
    return jax.shard_map(
        shards,
        mesh=mesh,
        in_specs=(
            P(None, "cuts", "row", None),
            P(),
            P(),
            P("cuts", "row"),
            P("cuts", "row"),
            P("cuts", "row"),
            P(),
        ),
        out_specs=(
            P(None, "cuts", "row", None),
            P("cuts", "row"),
            P("cuts", "row"),
            P(None, None, "cuts"),
        ),
        check_vma=False,
    )
```

time: 65.6 us -> 51.1 us (0.78)
  the two profiles are of different devices: /device:TPU:14 before, /device:TPU:25 now
where the time goes in v1:
time: 51.1 us; the launch traced here: 50.9 us
  Pallas kernels  50.3 us (98%)
  between operations  0.64 us (1%)
    pallas_call x1, Pallas kernels, shards(): pl.pallas_call(kernel, out_shape=(*results, jax.ShapeDtypeStruct((8, 8),...  48.5 us
    pallas_call x1, Pallas kernels, shards(): pl.pallas_call(hand_over, out_shape=(*results, jax.ShapeDtypeStruct((4, 2...  1.73 us

profile of v1, /device:TPU:25, one launch (start us, length us, event | category | flops | bytes accessed | tf_op | source)
XLA Modules:
  0.0 50.9 jit_solution(5721860834636275421)
XLA Ops:
  0.6 48.5 %shard_map.102 = (f32[2,8,16,256]{3,2,1,0:T(8,128)}, f32[8,512]{1,0:T(8,128)}, f32[8,512]{1,0:T(8,128)}, f32[8,8]{1,0:T(8,128)}) custom-call(s32[4]{0:T(128)} %shifts_in.1, f32[2,8,16,256]{3,2,1,0:T(8,128)} %field_in.1, f32[2,256,256]{2,1,0:T(8,128)} %row_in.1, f32[2,256,256]{2,1,0:T(8,128)} %col_in.1, f32[8,512]{1,0:T(8,128)} %phase_in.1, ...), custom_call_target="tpu_custom_call" | custom-call | tf_op jit(solution)/shard_map/pallas_call | solution.py:444
  49.2 1.7 %shard_map.103 = (f32[2,8,16,256]{3,2,1,0:T(8,128)}, f32[8,512]{1,0:T(8,128)}, f32[8,512]{1,0:T(8,128)}, f32[4,2,8]{2,1,0:T(2,128)}) custom-call(f32[2,8,16,256]{3,2,1,0:T(8,128)} %get-tuple-element.8.field, f32[8,512]{1,0:T(8,128)} %get-tuple-element.9.phase, f32[8,512]{1,0:T(8,128)} %get-tuple-element.10.energy, f32[8,8]{1,0:T(8,128)} %get-tuple-element.11.sums), custom_call_target="tpu_custom_call" | custom-call | tf_op jit(solution)/shard_map/pallas_call | solution.py:453

commit v2 on v1

--- a/solution.py
+++ b/solution.py
@@ -104,12 +104,6 @@
         remote(dst, dst, ss, rs, c, b).wait_recv()
 
     mark("start")
-    loads = [(phase_in, ph_in), (energy_in, en_in), (cells_in, ce_in), (field_in, own),
-             (col_in, colp), (row_in, rowp), (shifts_in, shifts)]
-    loads = [pltpu.make_async_copy(src, dst, lsem.at[n]) for n, (src, dst) in enumerate(loads)]
-    for copy in loads:
-        copy.start()
-
     barrier = pltpu.get_barrier_semaphore()
     below = (base_cut + 1) % CUTS
     itself = (half == h) & ((base_cut == c) | ((below == c) & (slot % 8 >= 6)))
@@ -129,16 +123,21 @@
     pl.semaphore_signal(barrier, inc=1, device_id=(partner, b), device_id_type=MESH)
     pl.semaphore_signal(barrier, inc=1, device_id=((c + CUTS - 1) % CUTS, b), device_id_type=MESH)
 
+    loads = [(phase_in, ph_in), (energy_in, en_in), (cells_in, ce_in), (field_in, own),
+             (col_in, colp), (row_in, rowp), (shifts_in, shifts)]
+    loads = [pltpu.make_async_copy(src, dst, lsem.at[n]) for n, (src, dst) in enumerate(loads)]
+    for copy in loads:
+        copy.start()
+
     mark("unpack")
     for n in (0, 1, 2):
         loads[n].wait()
     for u in range(8):
         for i in range(4):
             lanes = slice(128 * i, 128 * i + 128)
-            xel[u, i:i + 1, :] = ph_in[u:u + 1, lanes]
-            xel[u, 4 + i:5 + i, :] = en_in[u:u + 1, lanes]
-            xel[u, 8 + i:9 + i, :] = ce_in[u:u + 1, lanes].astype(F32)
-        xel[u, 12:16, :] = jnp.zeros((4, 128), F32)
+            xel[u, 0, i:i + 1, :] = ph_in[u:u + 1, lanes]
+            xel[u, 1, i:i + 1, :] = en_in[u:u + 1, lanes]
+            xel[u, 2, i:i + 1, :] = ce_in[u:u + 1, lanes].astype(F32)
 
     mark("w_barrier")
     loads[3].wait()
@@ -262,8 +261,8 @@
 
     def to_rows(source, dst, ss, rs):
         c1, c2 = (slot + 5) // 8, (slot + 8) // 8
-        for i in range(8):
-            v = (place + i) % 8
+        for q in (2, 6, 3, 7, 1, 5, 0, 4):
+            v = place ^ q
             for n, cc in ((0, c1), (1, c2)):
                 extra = None if n == 0 else c1 != c2
                 w = slot - 8 * cc + 8
@@ -286,32 +285,24 @@
     mark("first")
     one = shifts[0] == 1
     for v in range(8):
-        tile = jnp.where(one, rxel[0, v], rxel[1, v])
-        state[4 * v:4 * v + 4, :] = tile[0:4]
-        state[32 + 4 * v:36 + 4 * v, :] = tile[4:8]
-        cell_f[0, 4 * v:4 * v + 4, :] = tile[8:12]
+        state[4 * v:4 * v + 4, :] = jnp.where(one, rxel[0, v, 0], rxel[1, v, 0])
+        state[32 + 4 * v:36 + 4 * v, :] = jnp.where(one, rxel[0, v, 1], rxel[1, v, 1])
+        cell_f[0, 4 * v:4 * v + 4, :] = jnp.where(one, rxel[0, v, 2], rxel[1, v, 2])
     state[64:72, :] = jnp.zeros((8, 128), F32)
     build_onehot(0)
-    moved = 0
-    acc = None
+    moved = shifts[0]
+    mark("w_a2a")
+    for v in range(8):
+        await_from(arr.at[:, v], s_a2a.at[v], r_a2a.at[v], z * 2 + group, 8 * h + v)
+    fld[...] = jnp.where(((slot + moved) & 255) < shifts[0], 0.0, arr[...])
     for period in range(4):
-        one = shifts[period] == 1
-        moved = moved + shifts[period]
-        fresh = ((slot + moved) & 255) < shifts[period]
+        mark("samp")
+        sample()
         if period > 0:
             mark("w_st")
             for k in (1, 2):
                 sure_await(rst.at[period - 1, k - 1], s_st.at[period - 1, k - 1], r_st.at[period - 1, k - 1])
-            state[...] = jnp.where(one, rst[period - 1, 0], rst[period - 1, 1])
-        if period == 0:
-            mark("w_a2a")
-            for v in range(8):
-                await_from(arr.at[:, v], s_a2a.at[v], r_a2a.at[v], z * 2 + group, 8 * h + v)
-            fld[...] = jnp.where(fresh, 0.0, arr[...])
-        else:
-            fld[...] = jnp.where(fresh, 0.0, acc).reshape(2, 8, 16, 256)
-        mark("samp")
-        sample()
+            state[...] = jnp.where(shifts[period] == 1, rst[period - 1, 0], rst[period - 1, 1])
         mark("kick")
         phase, energy, total = kick(period)
         if period < 3:
@@ -349,10 +340,13 @@
         for part in range(2):
             sure_await(goth.at[period, part], s_ex.at[period, part], r_ex.at[period, part])
         mark("rowoth")
-        acc = acc + rows_of(1, goth[period].reshape(256, 256))
+        acc = (acc + rows_of(1, goth[period].reshape(256, 256))).reshape(2, 8, 16, 256)
+        if period < 3:
+            moved = moved + shifts[period + 1]
+            fld[...] = jnp.where(((slot + moved) & 255) < shifts[period + 1], 0.0, acc)
 
     mark("fsend")
-    fin[...] = acc.reshape(2, 8, 16, 256)
+    fin[...] = acc
     to_rows(lambda v: fin.at[:, v], rfld, s_fld, r_fld)
 
     mark("w_small")
@@ -431,7 +425,7 @@
         V(blocks, F32), V(blocks, F32), V((4, *blocks), F32), V((4, *blocks), F32),
         V((2, 32, 128), F32), V((4, 32, 128), F32), V((72, 128), F32), V((4, 32, 128), F32),
         pltpu.SMEM((4,), jnp.int32), V((8, 8), F32), V((8, 512), F32), V((8, 512), F32), V(blocks, F32),
-        V((8, 16, 128), F32), V((2, 8, 16, 128), F32), V((3, 72, 128), F32),
+        V((8, 3, 4, 128), F32), V((2, 8, 3, 4, 128), F32), V((3, 72, 128), F32),
         V((3, 2, 72, 128), F32), V((3, 2, 32, 128), F32), V((8, 128), F32), V((8, 128), F32),
         V((8, 16, 128), F32), V(blocks, F32), V((11, 2, 16, 256), F32), V((11, 16, 128), F32),
         D((11,)), D((8,)), D((8,)), D((2, 8)), D((2, 8)), D((4, 2)), D((4, 2)),

time: 51.1 us -> 50.3 us (0.984)
  the two profiles are of different devices: /device:TPU:25 before, /device:TPU:1 now
where the time goes in v2:
time: 50.3 us; the launch traced here: 50.1 us
  Pallas kernels  49.5 us (98%)
  between operations  0.64 us (1%)
    pallas_call x1, Pallas kernels, shards(): pl.pallas_call(kernel, out_shape=(*results, jax.ShapeDtypeStruct((8, 8),...  47.8 us
    pallas_call x1, Pallas kernels, shards(): pl.pallas_call(hand_over, out_shape=(*results, jax.ShapeDtypeStruct((4, 2...  1.73 us

profile of v2, /device:TPU:1, one launch (start us, length us, event | category | flops | bytes accessed | tf_op | source)
XLA Modules:
  0.0 50.1 jit_solution(6985277711330215723)
XLA Ops:
  0.6 47.8 %shard_map.102 = (f32[2,8,16,256]{3,2,1,0:T(8,128)}, f32[8,512]{1,0:T(8,128)}, f32[8,512]{1,0:T(8,128)}, f32[8,8]{1,0:T(8,128)}) custom-call(s32[4]{0:T(128)} %shifts_in.1, f32[2,8,16,256]{3,2,1,0:T(8,128)} %field_in.1, f32[2,256,256]{2,1,0:T(8,128)} %row_in.1, f32[2,256,256]{2,1,0:T(8,128)} %col_in.1, f32[8,512]{1,0:T(8,128)} %phase_in.1, ...), custom_call_target="tpu_custom_call" | custom-call | tf_op jit(solution)/shard_map/pallas_call | solution.py:438
  48.4 1.7 %shard_map.103 = (f32[2,8,16,256]{3,2,1,0:T(8,128)}, f32[8,512]{1,0:T(8,128)}, f32[8,512]{1,0:T(8,128)}, f32[4,2,8]{2,1,0:T(2,128)}) custom-call(f32[2,8,16,256]{3,2,1,0:T(8,128)} %get-tuple-element.8.field, f32[8,512]{1,0:T(8,128)} %get-tuple-element.9.phase, f32[8,512]{1,0:T(8,128)} %get-tuple-element.10.energy, f32[8,8]{1,0:T(8,128)} %get-tuple-element.11.sums), custom_call_target="tpu_custom_call" | custom-call | tf_op jit(solution)/shard_map/pallas_call | solution.py:447

commit v3 on v2

--- a/solution.py
+++ b/solution.py
@@ -48,7 +48,7 @@
            key_i, col_f, onehot, fld, arr, gown, goth, samp, emit, state, cell_f,
            shifts, out_sums, out_ph, out_en, out_fld, xel, rxel, sst, rst, rce, psum, psum_in, efin, fin, rfld, rel,
            lsem, s_a2a, r_a2a, s_xel, r_xel, s_ex, r_ex, s_st, r_st, s_ce, r_ce,
-           s_ps, r_ps, s_fld, r_fld, s_el, r_el):
+           s_ps, r_ps, s_fld, r_fld, s_el, r_el, go_first, go_relay):
     c = lax.axis_index("cuts")
     b = lax.axis_index("row")
     z = c // 2
@@ -116,10 +116,28 @@
                 pl.semaphore_signal(barrier, inc=1, device_id=(dc, 8 * h + v), device_id_type=MESH)
 
     greet(base_cut)
-    greet(below, slot % 8 >= 6)
+    greet(below, (slot % 8 >= 6) & (slot < SLOTS - 2))
     for k in (1, 2):
         pz, pb = chip_of((slot + k) % SLOTS)
-        pl.semaphore_signal(barrier, inc=1, device_id=(pz * 2 + h, pb), device_id_type=MESH)
+
+        @pl.when(slot + k < SLOTS)
+        def _():
+            pl.semaphore_signal(barrier, inc=1, device_id=(pz * 2 + h, pb), device_id_type=MESH)
+
+    for k in (1, 2):
+        pz, pb = chip_of(SLOTS - k)
+
+        @pl.when(c == 0)
+        def _():
+            pl.semaphore_signal(barrier, inc=1, device_id=(pz * 2 + half, pb), device_id_type=MESH)
+
+        for first in range(k):
+            qz, qb = chip_of(SLOTS + first - k)
+
+            @pl.when(slot == first)
+            def _():
+                pl.semaphore_signal(barrier, inc=1, device_id=(qz * 2 + h, qb), device_id_type=MESH)
+
     pl.semaphore_signal(barrier, inc=1, device_id=(partner, b), device_id_type=MESH)
     pl.semaphore_signal(barrier, inc=1, device_id=((c + CUTS - 1) % CUTS, b), device_id_type=MESH)
 
@@ -141,14 +159,30 @@
 
     mark("w_barrier")
     loads[3].wait()
-    pl.semaphore_wait(barrier, 14 - jnp.where(itself, 1, 0))
+    closing = jnp.where(slot == SLOTS - 1, 10, 0) + jnp.where(slot == SLOTS - 2, 9, 0)
+    opening = jnp.where(slot == 0, 2, 0) + jnp.where(slot == 1, 1, 0) + jnp.where(c == 0, 2, 0)
+    pl.semaphore_wait(barrier, 14 - jnp.where(itself, 1, 0) + closing - opening)
+
+    @pl.when(slot >= SLOTS - 2)
+    def _():
+        for v in range(8):
+            pl.semaphore_signal(go_first, inc=1, device_id=(0, 8 * h + v), device_id_type=MESH)
+        qz, qb = chip_of(0)
+        pl.semaphore_signal(go_relay, inc=1, device_id=(qz * 2 + h, qb), device_id_type=MESH)
+
+    @pl.when(slot == SLOTS - 1)
+    def _():
+        qz, qb = chip_of(1)
+        pl.semaphore_signal(go_relay, inc=1, device_id=(qz * 2 + h, qb), device_id_type=MESH)
+
 
     mark("send0")
     for i in range(8):
         u = (place + i) % 8
         for k in (1, 2):
             pz, pb = chip_of((8 * c + u - k + SLOTS) % SLOTS)
-            send(xel.at[u], rxel.at[k - 1, place], s_xel.at[k - 1, u], r_xel.at[k - 1, place], pz * 2 + half, pb)
+            send(xel.at[u], rxel.at[k - 1, place], s_xel.at[k - 1, u], r_xel.at[k - 1, place], pz * 2 + half, pb,
+                 jnp.logical_not((c == 0) & (u < k)))
     for i in range(8):
         u = (place + i) % 8
         _, db = chip_of(8 * c + u)
@@ -177,7 +211,7 @@
 
     def build_onehot(period):
         if period < 3:
-            relay(cell_f.at[period], rce, s_ce, r_ce, period)
+            relay(cell_f.at[period], rce, s_ce, r_ce, period, "inner" if period == 0 else None)
         cell = cell_f[period].astype(jnp.int32)
         key_i[...] = ((cell >> 8) & 15) + ((cell >> 7) & 1) * 16
         col_f[...] = (cell & 127).astype(F32)
@@ -188,9 +222,13 @@
                 col = jnp.broadcast_to(col_f[at:at + 1, :], (128, 128)).astype(BF16)
                 onehot[u, :, 128 * i:128 * i + 128] = jnp.where(iota == col, 1.0, 0.0).astype(BF16)
 
-    def relay(src, dst, ss, rs, period):
+    def relay(src, dst, ss, rs, period, when=None):
         for k in (1, 2):
             pz, pb = chip_of((slot - k + SLOTS) % SLOTS)
+            if when is not None:
+                send(src, dst.at[period, k - 1], ss.at[period, k - 1], rs.at[period, k - 1], pz * 2 + h, pb,
+                     (slot < k) if when == "closing" else (slot >= k))
+                continue
             sure_send(src, dst.at[period, k - 1], ss.at[period, k - 1], rs.at[period, k - 1], pz * 2 + h, pb)
 
     def sample():
@@ -290,6 +328,16 @@
         cell_f[0, 4 * v:4 * v + 4, :] = jnp.where(one, rxel[0, v, 2], rxel[1, v, 2])
     state[64:72, :] = jnp.zeros((8, 128), F32)
     build_onehot(0)
+    mark("wrap")
+
+    @pl.when(c == 0)
+    def _():
+        pl.semaphore_wait(go_first, 2)
+
+    for u, k in ((0, 1), (0, 2), (1, 2)):
+        pz, pb = chip_of(SLOTS + u - k)
+        send(xel.at[u], rxel.at[k - 1, place], s_xel.at[k - 1, u], r_xel.at[k - 1, place], pz * 2 + half, pb, c == 0)
+
     moved = shifts[0]
     mark("w_a2a")
     for v in range(8):
@@ -305,6 +353,13 @@
             state[...] = jnp.where(shifts[period] == 1, rst[period - 1, 0], rst[period - 1, 1])
         mark("kick")
         phase, energy, total = kick(period)
+        if period == 0:
+            for first in range(2):
+                @pl.when(slot == first)
+                def _():
+                    pl.semaphore_wait(go_relay, 2 - first)
+
+            relay(cell_f.at[0], rce, s_ce, r_ce, 0, "closing")
         if period < 3:
             sst[period, 0:32, :] = phase
             sst[period, 32:64, :] = energy
@@ -431,6 +486,7 @@
         D((11,)), D((8,)), D((8,)), D((2, 8)), D((2, 8)), D((4, 2)), D((4, 2)),
         D((3, 2)), D((3, 2)), D((3, 2)), D((3, 2)), D, D,
         D((2, 8)), D((11,)), D((2, 8)), D((11,)),
+        pltpu.SemaphoreType.REGULAR, pltpu.SemaphoreType.REGULAR,
     ]
     hbm = pl.BlockSpec(memory_space=pl.ANY)
     results = (jax.ShapeDtypeStruct(blocks, F32), jax.ShapeDtypeStruct((8, 512), F32),

time: 50.3 us -> 51.6 us (1.026)
  the two profiles are of different devices: /device:TPU:1 before, /device:TPU:4 now
where the time goes in v3:
time: 51.6 us; the launch traced here: 51.4 us
  Pallas kernels  50.7 us (98%)
  between operations  0.64 us (1%)
    pallas_call x1, Pallas kernels, shards(): pl.pallas_call(kernel, out_shape=(*results, jax.ShapeDtypeStruct((8, 8),...  49 us
    pallas_call x1, Pallas kernels, shards(): pl.pallas_call(hand_over, out_shape=(*results, jax.ShapeDtypeStruct((4, 2...  1.73 us

profile of v3, /device:TPU:4, one launch (start us, length us, event | category | flops | bytes accessed | tf_op | source)
XLA Modules:
  0.0 51.4 jit_solution(13510065817794206706)
XLA Ops:
  0.6 49.0 %shard_map.102 = (f32[2,8,16,256]{3,2,1,0:T(8,128)}, f32[8,512]{1,0:T(8,128)}, f32[8,512]{1,0:T(8,128)}, f32[8,8]{1,0:T(8,128)}) custom-call(s32[4]{0:T(128)} %shifts_in.1, f32[2,8,16,256]{3,2,1,0:T(8,128)} %field_in.1, f32[2,256,256]{2,1,0:T(8,128)} %row_in.1, f32[2,256,256]{2,1,0:T(8,128)} %col_in.1, f32[8,512]{1,0:T(8,128)} %phase_in.1, ...), custom_call_target="tpu_custom_call" | custom-call | tf_op jit(solution)/shard_map/pallas_call | solution.py:494
  49.6 1.7 %shard_map.103 = (f32[2,8,16,256]{3,2,1,0:T(8,128)}, f32[8,512]{1,0:T(8,128)}, f32[8,512]{1,0:T(8,128)}, f32[4,2,8]{2,1,0:T(2,128)}) custom-call(f32[2,8,16,256]{3,2,1,0:T(8,128)} %get-tuple-element.8.field, f32[8,512]{1,0:T(8,128)} %get-tuple-element.9.phase, f32[8,512]{1,0:T(8,128)} %get-tuple-element.10.energy, f32[8,8]{1,0:T(8,128)} %get-tuple-element.11.sums), custom_call_target="tpu_custom_call" | custom-call | tf_op jit(solution)/shard_map/pallas_call | solution.py:503

commit v4 on v2

--- a/solution.py
+++ b/solution.py
@@ -121,7 +121,6 @@
         pz, pb = chip_of((slot + k) % SLOTS)
         pl.semaphore_signal(barrier, inc=1, device_id=(pz * 2 + h, pb), device_id_type=MESH)
     pl.semaphore_signal(barrier, inc=1, device_id=(partner, b), device_id_type=MESH)
-    pl.semaphore_signal(barrier, inc=1, device_id=((c + CUTS - 1) % CUTS, b), device_id_type=MESH)
 
     loads = [(phase_in, ph_in), (energy_in, en_in), (cells_in, ce_in), (field_in, own),
              (col_in, colp), (row_in, rowp), (shifts_in, shifts)]
@@ -141,7 +140,7 @@
 
     mark("w_barrier")
     loads[3].wait()
-    pl.semaphore_wait(barrier, 14 - jnp.where(itself, 1, 0))
+    pl.semaphore_wait(barrier, 13 - jnp.where(itself, 1, 0))
 
     mark("send0")
     for i in range(8):
@@ -330,11 +329,14 @@
         else:
             mark("elsend")
             sure_await(psum_in, s_ps, r_ps)
-            total = psum[...] + psum_in[...]
+            diagonal = (lax.broadcasted_iota(jnp.int32, (8, 128), 0)
+                        == lax.broadcasted_iota(jnp.int32, (8, 128), 1))
+            total = jnp.sum(psum[...] + psum_in[...], axis=1, keepdims=True)
+            total = jnp.sum(jnp.where(diagonal, total, 0.0), axis=0, keepdims=True)
             for v in range(8):
                 efin[v, 0:4, :] = state[4 * v:4 * v + 4, :]
                 efin[v, 4:8, :] = state[32 + 4 * v:36 + 4 * v, :]
-                efin[v, 8:16, :] = total
+                efin[v, 8:9, :] = total
             to_rows(lambda v: efin.at[v], rel, s_el, r_el)
         mark("w_ex")
         for part in range(2):
@@ -364,7 +366,8 @@
             lanes = slice(128 * i, 128 * i + 128)
             out_ph[u:u + 1, lanes] = tile[i:i + 1]
             out_en[u:u + 1, lanes] = tile[4 + i:5 + i]
-        sums = jnp.where(lane == u, jnp.sum(tile[8:16], axis=1, keepdims=True), sums)
+        total = jnp.sum(jnp.where(diagonal, tile[8:9], 0.0), axis=1, keepdims=True)
+        sums = jnp.where(lane == u, total, sums)
     out_sums[...] = sums * ELEC ** (-0.5)
     stores = [(out_ph, phase_out), (out_en, energy_out), (out_sums, sums_out), (out_fld, field_out)]
     stores = [pltpu.make_async_copy(src, dst, lsem.at[7 + n]) for n, (src, dst) in enumerate(stores)]
@@ -427,7 +430,7 @@
         pltpu.SMEM((4,), jnp.int32), V((8, 8), F32), V((8, 512), F32), V((8, 512), F32), V(blocks, F32),
         V((8, 3, 4, 128), F32), V((2, 8, 3, 4, 128), F32), V((3, 72, 128), F32),
         V((3, 2, 72, 128), F32), V((3, 2, 32, 128), F32), V((8, 128), F32), V((8, 128), F32),
-        V((8, 16, 128), F32), V(blocks, F32), V((11, 2, 16, 256), F32), V((11, 16, 128), F32),
+        V((8, 9, 128), F32), V(blocks, F32), V((11, 2, 16, 256), F32), V((11, 9, 128), F32),
         D((11,)), D((8,)), D((8,)), D((2, 8)), D((2, 8)), D((4, 2)), D((4, 2)),
         D((3, 2)), D((3, 2)), D((3, 2)), D((3, 2)), D, D,
         D((2, 8)), D((11,)), D((2, 8)), D((11,)),

time: 50.3 us -> 49.7 us (0.988)
  Pallas kernels: 49.5 us -> 48.9 us
    pallas_call x1, Pallas kernels: 47.8 us -> 47.1 us  [shards(): pl.pallas_call(kernel, out_shape=(*results, jax.ShapeDtypeStruct((8, 8),...]
where the time goes in v4:
time: 49.7 us; the launch traced here: 49.5 us
  Pallas kernels  48.9 us (98%)
  between operations  0.64 us (1%)
    pallas_call x1, Pallas kernels, shards(): pl.pallas_call(kernel, out_shape=(*results, jax.ShapeDtypeStruct((8, 8),...  47.1 us
    pallas_call x1, Pallas kernels, shards(): pl.pallas_call(hand_over, out_shape=(*results, jax.ShapeDtypeStruct((4, 2...  1.73 us

profile of v4, /device:TPU:1, one launch (start us, length us, event | category | flops | bytes accessed | tf_op | source)
XLA Modules:
  0.0 49.5 jit_solution(850298177434720283)
XLA Ops:
  0.6 47.1 %shard_map.102 = (f32[2,8,16,256]{3,2,1,0:T(8,128)}, f32[8,512]{1,0:T(8,128)}, f32[8,512]{1,0:T(8,128)}, f32[8,8]{1,0:T(8,128)}) custom-call(s32[4]{0:T(128)} %shifts_in.1, f32[2,8,16,256]{3,2,1,0:T(8,128)} %field_in.1, f32[2,256,256]{2,1,0:T(8,128)} %row_in.1, f32[2,256,256]{2,1,0:T(8,128)} %col_in.1, f32[8,512]{1,0:T(8,128)} %phase_in.1, ...), custom_call_target="tpu_custom_call" | custom-call | tf_op jit(solution)/shard_map/pallas_call | solution.py:441
  47.8 1.7 %shard_map.103 = (f32[2,8,16,256]{3,2,1,0:T(8,128)}, f32[8,512]{1,0:T(8,128)}, f32[8,512]{1,0:T(8,128)}, f32[4,2,8]{2,1,0:T(2,128)}) custom-call(f32[2,8,16,256]{3,2,1,0:T(8,128)} %get-tuple-element.8.field, f32[8,512]{1,0:T(8,128)} %get-tuple-element.9.phase, f32[8,512]{1,0:T(8,128)} %get-tuple-element.10.energy, f32[8,8]{1,0:T(8,128)} %get-tuple-element.11.sums), custom_call_target="tpu_custom_call" | custom-call | tf_op jit(solution)/shard_map/pallas_call | solution.py:450

commit v5 on v4

--- a/solution.py
+++ b/solution.py
@@ -45,7 +45,7 @@
 def kernel(shifts_in, field_in, row_in, col_in, phase_in, energy_in, cells_in,
            field_out, phase_out, energy_out, sums_out,
            own, rowp, colp, ph_in, en_in, ce_in, mh, ml, ah, al,
-           key_i, col_f, onehot, fld, arr, gown, goth, samp, emit, state, cell_f,
+           key_i, col_i, onehot, fld, arr, gown, goth, samp, emit, state, cell_f,
            shifts, out_sums, out_ph, out_en, out_fld, xel, rxel, sst, rst, rce, psum, psum_in, efin, fin, rfld, rel,
            lsem, s_a2a, r_a2a, s_xel, r_xel, s_ex, r_ex, s_st, r_st, s_ce, r_ce,
            s_ps, r_ps, s_fld, r_fld, s_el, r_el):
@@ -179,13 +179,13 @@
             relay(cell_f.at[period], rce, s_ce, r_ce, period)
         cell = cell_f[period].astype(jnp.int32)
         key_i[...] = ((cell >> 8) & 15) + ((cell >> 7) & 1) * 16
-        col_f[...] = (cell & 127).astype(F32)
-        iota = lax.broadcasted_iota(jnp.int32, (128, 128), 0).astype(F32).astype(BF16)
+        col_i[...] = cell & 127
+        iota = lax.broadcasted_iota(jnp.int32, (128, 128), 0)
         for u in range(8):
             for i in range(4):
                 at = 4 * u + i
-                col = jnp.broadcast_to(col_f[at:at + 1, :], (128, 128)).astype(BF16)
-                onehot[u, :, 128 * i:128 * i + 128] = jnp.where(iota == col, 1.0, 0.0).astype(BF16)
+                hot = jnp.where(iota == col_i[at:at + 1, :], 1.0, 0.0)
+                onehot[u, :, 128 * i:128 * i + 128] = hot.astype(BF16)
 
     def relay(src, dst, ss, rs, period):
         for k in (1, 2):
@@ -424,7 +424,7 @@
         V(blocks, F32), V(square, F32), V(square, F32),
         V((8, 512), F32), V((8, 512), F32), V((8, 512), jnp.int32),
         V((512, 512), BF16), V((512, 512), BF16), V(square, BF16), V(square, BF16),
-        V((32, 128), jnp.int32), V((32, 128), F32), V((8, 128, 512), BF16),
+        V((32, 128), jnp.int32), V((32, 128), jnp.int32), V((8, 128, 512), BF16),
         V(blocks, F32), V(blocks, F32), V((4, *blocks), F32), V((4, *blocks), F32),
         V((2, 32, 128), F32), V((4, 32, 128), F32), V((72, 128), F32), V((4, 32, 128), F32),
         pltpu.SMEM((4,), jnp.int32), V((8, 8), F32), V((8, 512), F32), V((8, 512), F32), V(blocks, F32),

time: 49.7 us -> 49.7 us (level)
  no operation moved by 1% of the time
where the time goes in v5:
time: 49.7 us; the launch traced here: 49.5 us
  Pallas kernels  48.9 us (98%)
  between operations  0.64 us (1%)
    pallas_call x1, Pallas kernels, shards(): pl.pallas_call(kernel, out_shape=(*results, jax.ShapeDtypeStruct((8, 8),...  47.2 us
    pallas_call x1, Pallas kernels, shards(): pl.pallas_call(hand_over, out_shape=(*results, jax.ShapeDtypeStruct((4, 2...  1.73 us

profile of v5, /device:TPU:1, one launch (start us, length us, event | category | flops | bytes accessed | tf_op | source)
XLA Modules:
  0.0 49.5 jit_solution(10058910640334208079)
XLA Ops:
  0.6 47.2 %shard_map.102 = (f32[2,8,16,256]{3,2,1,0:T(8,128)}, f32[8,512]{1,0:T(8,128)}, f32[8,512]{1,0:T(8,128)}, f32[8,8]{1,0:T(8,128)}) custom-call(s32[4]{0:T(128)} %shifts_in.1, f32[2,8,16,256]{3,2,1,0:T(8,128)} %field_in.1, f32[2,256,256]{2,1,0:T(8,128)} %row_in.1, f32[2,256,256]{2,1,0:T(8,128)} %col_in.1, f32[8,512]{1,0:T(8,128)} %phase_in.1, ...), custom_call_target="tpu_custom_call" | custom-call | tf_op jit(solution)/shard_map/pallas_call | solution.py:441
  47.8 1.7 %shard_map.103 = (f32[2,8,16,256]{3,2,1,0:T(8,128)}, f32[8,512]{1,0:T(8,128)}, f32[8,512]{1,0:T(8,128)}, f32[4,2,8]{2,1,0:T(2,128)}) custom-call(f32[2,8,16,256]{3,2,1,0:T(8,128)} %get-tuple-element.8.field, f32[8,512]{1,0:T(8,128)} %get-tuple-element.9.phase, f32[8,512]{1,0:T(8,128)} %get-tuple-element.10.energy, f32[8,8]{1,0:T(8,128)} %get-tuple-element.11.sums), custom_call_target="tpu_custom_call" | custom-call | tf_op jit(solution)/shard_map/pallas_call | solution.py:450

commit v6 on v5

--- a/solution.py
+++ b/solution.py
@@ -43,10 +43,10 @@
 
 
 def kernel(shifts_in, field_in, row_in, col_in, phase_in, energy_in, cells_in,
-           field_out, phase_out, energy_out, sums_out,
+           rfld, rel,
            own, rowp, colp, ph_in, en_in, ce_in, mh, ml, ah, al,
            key_i, col_i, onehot, fld, arr, gown, goth, samp, emit, state, cell_f,
-           shifts, out_sums, out_ph, out_en, out_fld, xel, rxel, sst, rst, rce, psum, psum_in, efin, fin, rfld, rel,
+           shifts, xel, rxel, sst, rst, rce, psum, psum_in, efin, fin,
            lsem, s_a2a, r_a2a, s_xel, r_xel, s_ex, r_ex, s_st, r_st, s_ce, r_ce,
            s_ps, r_ps, s_fld, r_fld, s_el, r_el):
     c = lax.axis_index("cuts")
@@ -74,7 +74,7 @@
             src_ref=src, dst_ref=dst, send_sem=ss, recv_sem=rs,
             device_id=(dc, db), device_id_type=MESH)
 
-    def send(src, dst, ss, rs, dc, db, extra=None):
+    def send(src, dst, ss, rs, dc, db, extra=None, far=True):
         here = (dc == c) & (db == b)
         there = jnp.logical_not(here)
         if extra is not None:
@@ -87,7 +87,10 @@
 
         @pl.when(here)
         def _():
-            dst[...] = src[...]
+            if far:
+                dst[...] = src[...]
+            else:
+                pltpu.make_async_copy(src, dst, rs).start()
 
         sends.append((there, src, dst, ss, rs))
 
@@ -265,7 +268,7 @@
             for n, cc in ((0, c1), (1, c2)):
                 extra = None if n == 0 else c1 != c2
                 w = slot - 8 * cc + 8
-                send(source(v), dst.at[w], ss.at[n, v], rs.at[w], cc % CUTS, 8 * h + v, extra)
+                send(source(v), dst.at[w], ss.at[n, v], rs.at[w], cc % CUTS, 8 * h + v, extra, False)
 
     def cells_for(period):
         mark("w_ce")
@@ -353,12 +356,40 @@
 
     mark("w_small")
     for w in range(11):
-        j = (8 * c - 8 + w + SLOTS) % SLOTS
-        pz, pb = chip_of(j)
-        await_from(rel.at[w], s_el.at[0, 0], r_el.at[w], pz * 2 + half, pb)
-    mark("smallout")
-    base = jnp.clip(8 - moved, 0, 3)
+        sure_await(rel.at[w], s_el.at[0, 0], r_el.at[w])
+    mark("w_fld")
+    for w in range(11):
+        sure_await(rfld.at[w], s_fld.at[0, 0], r_fld.at[w])
+
+    mark("drain")
+    for there, src, dst, ss, rs in sends:
+        copy = remote(src, dst, ss, rs, c, b)
+        if there is None:
+            copy.wait_send()
+        else:
+            @pl.when(there)
+            def _():
+                copy.wait_send()
+    mark(None)
+
+
+def hand_over(shifts_in, fields, electrons, field_out, phase_out, energy_out, bunching_out,
+              shifts, rfld, rel, out_fld, out_ph, out_en, out_sums, bunching, sem):
+    ins = [(shifts_in, shifts), (electrons, rel), (fields, rfld)]
+    outs = [(out_ph, phase_out), (out_en, energy_out), (bunching, bunching_out), (out_fld, field_out)]
+    ins = [pltpu.make_async_copy(src, dst, sem.at[n]) for n, (src, dst) in enumerate(ins)]
+    outs = [pltpu.make_async_copy(src, dst, sem.at[3 + n]) for n, (src, dst) in enumerate(outs)]
+    for copy in ins:
+        copy.start()
+    for copy in ins:
+        copy.wait()
+    base = jnp.clip(8 - (shifts[0] + shifts[1] + shifts[2] + shifts[3]), 0, 3)
+    for u in range(8):
+        out_fld[:, u] = rfld[base + u]
+    outs[3].start()
     lane = lax.broadcasted_iota(jnp.int32, (8, 8), 1)
+    diagonal = (lax.broadcasted_iota(jnp.int32, (8, 128), 0)
+                == lax.broadcasted_iota(jnp.int32, (8, 128), 1))
     sums = jnp.zeros((8, 8), F32)
     for u in range(8):
         tile = rel[base + u]
@@ -369,48 +400,10 @@
         total = jnp.sum(jnp.where(diagonal, tile[8:9], 0.0), axis=1, keepdims=True)
         sums = jnp.where(lane == u, total, sums)
     out_sums[...] = sums * ELEC ** (-0.5)
-    stores = [(out_ph, phase_out), (out_en, energy_out), (out_sums, sums_out), (out_fld, field_out)]
-    stores = [pltpu.make_async_copy(src, dst, lsem.at[7 + n]) for n, (src, dst) in enumerate(stores)]
-    for copy in stores[:3]:
+    for period in range(4):
+        bunching[period] = out_sums[2 * period:2 * period + 2]
+    for copy in outs[:3]:
         copy.start()
-    mark("w_fld")
-    for w in range(11):
-        j = (8 * c - 8 + w + SLOTS) % SLOTS
-        pz, pb = chip_of(j)
-        await_from(rfld.at[w], s_fld.at[0, 0], r_fld.at[w], pz * 2 + half, pb)
-    mark("fout")
-    for u in range(8):
-        out_fld[:, u] = rfld[base + u]
-    stores[3].start()
-
-    mark("drain")
-    for there, src, dst, ss, rs in sends:
-        copy = remote(src, dst, ss, rs, c, b)
-        if there is None:
-            copy.wait_send()
-        else:
-            @pl.when(there)
-            def _():
-                copy.wait_send()
-    for copy in stores:
-        copy.wait()
-    mark(None)
-
-
-def hand_over(field, phase, energy, sums, field_out, phase_out, energy_out, bunching_out,
-              a, p, e, q, out, sem):
-    ins = [(field, a), (phase, p), (energy, e), (sums, q)]
-    outs = [(a, field_out), (p, phase_out), (e, energy_out), (out, bunching_out)]
-    ins = [pltpu.make_async_copy(src, dst, sem.at[n]) for n, (src, dst) in enumerate(ins)]
-    outs = [pltpu.make_async_copy(src, dst, sem.at[4 + n]) for n, (src, dst) in enumerate(outs)]
-    for copy in ins:
-        copy.start()
-    for n in (3, 1, 2, 0):
-        ins[n].wait()
-        if n == 3:
-            for period in range(4):
-                out[period] = q[2 * period:2 * period + 2]
-        outs[n].start()
     for copy in outs:
         copy.wait()
 
@@ -427,10 +420,10 @@
         V((32, 128), jnp.int32), V((32, 128), jnp.int32), V((8, 128, 512), BF16),
         V(blocks, F32), V(blocks, F32), V((4, *blocks), F32), V((4, *blocks), F32),
         V((2, 32, 128), F32), V((4, 32, 128), F32), V((72, 128), F32), V((4, 32, 128), F32),
-        pltpu.SMEM((4,), jnp.int32), V((8, 8), F32), V((8, 512), F32), V((8, 512), F32), V(blocks, F32),
+        pltpu.SMEM((4,), jnp.int32),
         V((8, 3, 4, 128), F32), V((2, 8, 3, 4, 128), F32), V((3, 72, 128), F32),
         V((3, 2, 72, 128), F32), V((3, 2, 32, 128), F32), V((8, 128), F32), V((8, 128), F32),
-        V((8, 9, 128), F32), V(blocks, F32), V((11, 2, 16, 256), F32), V((11, 9, 128), F32),
+        V((8, 9, 128), F32), V(blocks, F32),
         D((11,)), D((8,)), D((8,)), D((2, 8)), D((2, 8)), D((4, 2)), D((4, 2)),
         D((3, 2)), D((3, 2)), D((3, 2)), D((3, 2)), D, D,
         D((2, 8)), D((11,)), D((2, 8)), D((11,)),
@@ -440,9 +433,9 @@
                jax.ShapeDtypeStruct((8, 512), F32))
     out = pl.pallas_call(
         kernel,
-        out_shape=(*results, jax.ShapeDtypeStruct((8, 8), F32)),
+        out_shape=(jax.ShapeDtypeStruct((11, 2, 16, 256), F32), jax.ShapeDtypeStruct((11, 9, 128), F32)),
         in_specs=[hbm] * 7,
-        out_specs=[hbm] * 4,
+        out_specs=[hbm] * 2,
         scratch_shapes=scratch,
         compiler_params=pltpu.CompilerParams(
             collective_id=0, has_side_effects=True, vmem_limit_bytes=VMEM_LIMIT),
@@ -450,12 +443,13 @@
     return pl.pallas_call(
         hand_over,
         out_shape=(*results, jax.ShapeDtypeStruct((4, 2, 8), F32)),
-        in_specs=[hbm] * 4,
+        in_specs=[hbm] * 3,
         out_specs=[hbm] * 4,
-        scratch_shapes=[V(blocks, F32), V((8, 512), F32), V((8, 512), F32), V((8, 8), F32),
-                        V((4, 2, 8), F32), D((8,))],
+        scratch_shapes=[pltpu.SMEM((4,), jnp.int32), V((11, 2, 16, 256), F32), V((11, 9, 128), F32),
+                        V(blocks, F32), V((8, 512), F32), V((8, 512), F32), V((8, 8), F32),
+                        V((4, 2, 8), F32), D((7,))],
         compiler_params=pltpu.CompilerParams(vmem_limit_bytes=VMEM_LIMIT),
-    )(*out)
+    )(shifts, *out)
 
 
 def solution(mesh):

time: 49.7 us -> 49.4 us (level)
  no operation moved by 1% of the time
where the time goes in v6:
time: 49.4 us; the launch traced here: 49.2 us
  Pallas kernels  48.6 us (98%)
  between operations  0.64 us (1%)
    pallas_call x1, Pallas kernels, shards(): pl.pallas_call(kernel, out_shape=(jax.ShapeDtypeStruct((11, 2, 16, 256),...  46.7 us
    pallas_call x1, Pallas kernels, shards(): pl.pallas_call(hand_over, out_shape=(*results, jax.ShapeDtypeStruct((4, 2...  1.82 us

profile of v6, /device:TPU:1, one launch (start us, length us, event | category | flops | bytes accessed | tf_op | source)
XLA Modules:
  0.0 49.2 jit_solution(2309607802193363638)
XLA Ops:
  0.6 46.7 %shard_map.102 = (f32[11,2,16,256]{3,2,1,0:T(8,128)}, f32[11,9,128]{2,1,0:T(8,128)}) custom-call(s32[4]{0:T(128)} %shifts_in.3, f32[2,8,16,256]{3,2,1,0:T(8,128)} %field_in.1, f32[2,256,256]{2,1,0:T(8,128)} %row_in.1, f32[2,256,256]{2,1,0:T(8,128)} %col_in.1, f32[8,512]{1,0:T(8,128)} %phase_in.1, f32[8,512]{1,0:T(8,128)} %energy_in.1, s32[8,512]{1,0:T(8,128)} %cells_in.1), custom_call_target="tpu_custom_call" | custom-call | tf_op jit(solution)/shard_map/pallas_call | solution.py:434
  47.4 1.8 %shard_map.103 = (f32[2,8,16,256]{3,2,1,0:T(8,128)}, f32[8,512]{1,0:T(8,128)}, f32[8,512]{1,0:T(8,128)}, f32[4,2,8]{2,1,0:T(2,128)}) custom-call(s32[4]{0:T(128)} %shifts_in.3, f32[11,2,16,256]{3,2,1,0:T(8,128)} %get-tuple-element.6.fields, f32[11,9,128]{2,1,0:T(8,128)} %get-tuple-element.7.electrons), custom_call_target="tpu_custom_call" | custom-call | tf_op jit(solution)/shard_map/pallas_call | solution.py:443

commit v7 on v6

--- a/solution.py
+++ b/solution.py
@@ -191,7 +191,7 @@
                 onehot[u, :, 128 * i:128 * i + 128] = hot.astype(BF16)
 
     def relay(src, dst, ss, rs, period):
-        for k in (1, 2):
+        for k in (2, 1):
             pz, pb = chip_of((slot - k + SLOTS) % SLOTS)
             sure_send(src, dst.at[period, k - 1], ss.at[period, k - 1], rs.at[period, k - 1], pz * 2 + h, pb)
 
@@ -265,7 +265,7 @@
         c1, c2 = (slot + 5) // 8, (slot + 8) // 8
         for q in (2, 6, 3, 7, 1, 5, 0, 4):
             v = place ^ q
-            for n, cc in ((0, c1), (1, c2)):
+            for n, cc in ((1, c2), (0, c1)):
                 extra = None if n == 0 else c1 != c2
                 w = slot - 8 * cc + 8
                 send(source(v), dst.at[w], ss.at[n, v], rs.at[w], cc % CUTS, 8 * h + v, extra, False)
@@ -381,12 +381,9 @@
     outs = [pltpu.make_async_copy(src, dst, sem.at[3 + n]) for n, (src, dst) in enumerate(outs)]
     for copy in ins:
         copy.start()
-    for copy in ins:
-        copy.wait()
+    ins[0].wait()
+    ins[1].wait()
     base = jnp.clip(8 - (shifts[0] + shifts[1] + shifts[2] + shifts[3]), 0, 3)
-    for u in range(8):
-        out_fld[:, u] = rfld[base + u]
-    outs[3].start()
     lane = lax.broadcasted_iota(jnp.int32, (8, 8), 1)
     diagonal = (lax.broadcasted_iota(jnp.int32, (8, 128), 0)
                 == lax.broadcasted_iota(jnp.int32, (8, 128), 1))
@@ -404,6 +401,10 @@
         bunching[period] = out_sums[2 * period:2 * period + 2]
     for copy in outs[:3]:
         copy.start()
+    ins[2].wait()
+    for u in range(8):
+        out_fld[:, u] = rfld[base + u]
+    outs[3].start()
     for copy in outs:
         copy.wait()
 

time: 49.4 us -> 49 us (level)
  Pallas kernels: 48.6 us -> 48.1 us
where the time goes in v7:
time: 49 us; the launch traced here: 48.8 us
  Pallas kernels  48.1 us (98%)
  between operations  0.64 us (1%)
    pallas_call x1, Pallas kernels, shards(): pl.pallas_call(kernel, out_shape=(jax.ShapeDtypeStruct((11, 2, 16, 256),...  46.3 us
    pallas_call x1, Pallas kernels, shards(): pl.pallas_call(hand_over, out_shape=(*results, jax.ShapeDtypeStruct((4, 2...  1.8 us

profile of v7, /device:TPU:1, one launch (start us, length us, event | category | flops | bytes accessed | tf_op | source)
XLA Modules:
  0.0 48.8 jit_solution(2554324829871159694)
XLA Ops:
  0.6 46.3 %shard_map.102 = (f32[11,2,16,256]{3,2,1,0:T(8,128)}, f32[11,9,128]{2,1,0:T(8,128)}) custom-call(s32[4]{0:T(128)} %shifts_in.3, f32[2,8,16,256]{3,2,1,0:T(8,128)} %field_in.1, f32[2,256,256]{2,1,0:T(8,128)} %row_in.1, f32[2,256,256]{2,1,0:T(8,128)} %col_in.1, f32[8,512]{1,0:T(8,128)} %phase_in.1, f32[8,512]{1,0:T(8,128)} %energy_in.1, s32[8,512]{1,0:T(8,128)} %cells_in.1), custom_call_target="tpu_custom_call" | custom-call | tf_op jit(solution)/shard_map/pallas_call | solution.py:435
  47.0 1.8 %shard_map.103 = (f32[2,8,16,256]{3,2,1,0:T(8,128)}, f32[8,512]{1,0:T(8,128)}, f32[8,512]{1,0:T(8,128)}, f32[4,2,8]{2,1,0:T(2,128)}) custom-call(s32[4]{0:T(128)} %shifts_in.3, f32[11,2,16,256]{3,2,1,0:T(8,128)} %get-tuple-element.6.fields, f32[11,9,128]{2,1,0:T(8,128)} %get-tuple-element.7.electrons), custom_call_target="tpu_custom_call" | custom-call | tf_op jit(solution)/shard_map/pallas_call | solution.py:444

commit v8 on v7

--- a/solution.py
+++ b/solution.py
@@ -118,8 +118,8 @@
             def _():
                 pl.semaphore_signal(barrier, inc=1, device_id=(dc, 8 * h + v), device_id_type=MESH)
 
+    greet(below, slot % 8 >= 6)
     greet(base_cut)
-    greet(below, slot % 8 >= 6)
     for k in (1, 2):
         pz, pb = chip_of((slot + k) % SLOTS)
         pl.semaphore_signal(barrier, inc=1, device_id=(pz * 2 + h, pb), device_id_type=MESH)
@@ -148,7 +148,7 @@
     mark("send0")
     for i in range(8):
         u = (place + i) % 8
-        for k in (1, 2):
+        for k in (2, 1):
             pz, pb = chip_of((8 * c + u - k + SLOTS) % SLOTS)
             send(xel.at[u], rxel.at[k - 1, place], s_xel.at[k - 1, u], r_xel.at[k - 1, place], pz * 2 + half, pb)
     for i in range(8):

time: 49 us -> 49.1 us (level)
  no operation moved by 1% of the time
where the time goes in v8:
time: 49.1 us; the launch traced here: 48.9 us
  Pallas kernels  48.2 us (98%)
  between operations  0.64 us (1%)
    pallas_call x1, Pallas kernels, shards(): pl.pallas_call(kernel, out_shape=(jax.ShapeDtypeStruct((11, 2, 16, 256),...  46.4 us
    pallas_call x1, Pallas kernels, shards(): pl.pallas_call(hand_over, out_shape=(*results, jax.ShapeDtypeStruct((4, 2...  1.8 us

profile of v8, /device:TPU:1, one launch (start us, length us, event | category | flops | bytes accessed | tf_op | source)
XLA Modules:
  0.0 48.9 jit_solution(7009759441493706945)
XLA Ops:
  0.6 46.4 %shard_map.102 = (f32[11,2,16,256]{3,2,1,0:T(8,128)}, f32[11,9,128]{2,1,0:T(8,128)}) custom-call(s32[4]{0:T(128)} %shifts_in.3, f32[2,8,16,256]{3,2,1,0:T(8,128)} %field_in.1, f32[2,256,256]{2,1,0:T(8,128)} %row_in.1, f32[2,256,256]{2,1,0:T(8,128)} %col_in.1, f32[8,512]{1,0:T(8,128)} %phase_in.1, f32[8,512]{1,0:T(8,128)} %energy_in.1, s32[8,512]{1,0:T(8,128)} %cells_in.1), custom_call_target="tpu_custom_call" | custom-call | tf_op jit(solution)/shard_map/pallas_call | solution.py:435
  47.1 1.8 %shard_map.103 = (f32[2,8,16,256]{3,2,1,0:T(8,128)}, f32[8,512]{1,0:T(8,128)}, f32[8,512]{1,0:T(8,128)}, f32[4,2,8]{2,1,0:T(2,128)}) custom-call(s32[4]{0:T(128)} %shifts_in.3, f32[11,2,16,256]{3,2,1,0:T(8,128)} %get-tuple-element.6.fields, f32[11,9,128]{2,1,0:T(8,128)} %get-tuple-element.7.electrons), custom_call_target="tpu_custom_call" | custom-call | tf_op jit(solution)/shard_map/pallas_call | solution.py:444
